TPU v7x, 32 devices: a whole 2x2x4 slice. The times are simulated.
32 devices in a mesh: node: 8 (over y, x, core), stripe: 4 (over z).
Axes of the slice: x: 2, y: 2, z: 4, core: 2. Of those that a mesh axis runs over, the one named last changes fastest.
Arguments:
- groups: bfloat16 [4, 16, 256, 8, 512], P('stripe', 'node'), may hold values from -21 to 21
- gamma: float32 [8, 8], replicated, may hold values from -2 to 2
- coeffs: float32 [4, 12, 8, 8], replicated, may hold values from -0.625 to 0.625
Outputs:
- syndrome: float32 [256, 4, 4, 8, 512], P('node', 'stripe')
- scores: float32 [256, 4, 4], P('node', 'stripe')
All inputs are finite; a program needn't handle non-finite values.
Results may differ from a plain program's by a relative error of at most 0.0003.
Values may be sent and summed in bfloat16 or wider, within the bound.
No kernel may reach another device: no remote copies, remote signals or barrier semaphores. Data moves between devices by JAX's collectives and lax.ppermute only.
A program may use at most 64 MiB of HBM per device.

v0:
```python
import jax
import jax.numpy as jnp
from jax import lax
from jax.sharding import PartitionSpec as P

LAYERS = 256
PLANES = 8
PARITY = 4
DATA_NODES = 12
VIRTUAL = 2


precise = lax.Precision.HIGHEST
epsilon = 1e-06


def for_sending(x):
    return jax.tree.map(lambda a: a.astype(jnp.bfloat16) if a.dtype == jnp.float32 else a, x)


def from_behind(block, axis, distance):
    devices = range(lax.axis_size(axis))
    route = [((i - distance) % len(devices), i) for i in devices]
    return lax.ppermute(block, axis, route)


def mix_planes(matrix, values):
    return jnp.einsum("pq,...qb->...pb", matrix, values, precision=precise)


def inverse_factor(gamma):
    order_count = gamma.shape[0]
    identity = jnp.eye(order_count, dtype=jnp.float32)
    mixed = identity + jnp.dot(gamma.T, gamma, precision=precise)
    factor = jnp.linalg.cholesky(mixed)
    solved_rows = []
    for row_at in range(order_count):
        running = identity[row_at]
        for earlier in range(row_at):
            running = running - factor[row_at, earlier] * solved_rows[earlier]
        solved_rows.append(running / factor[row_at, row_at])
    solved = jnp.stack(solved_rows)
    return jnp.dot(solved.T, solved, precision=precise)


def to_front(values, digit_axis):

    def to_mover(position):
        return lambda operand: jnp.moveaxis(operand, 4 - position, 1)

    return lax.switch(digit_axis, [to_mover(position) for position in range(4)], values)


def from_front(values, digit_axis):

    def from_mover(position):
        return lambda operand: jnp.moveaxis(operand, 1, 4 - position)

    return lax.switch(digit_axis, [from_mover(position) for position in range(4)], values)


def local(groups, gamma, coeffs):
    stripes_here = groups.shape[0]
    nodes_here = groups.shape[1]
    byte_count = groups.shape[4]
    device = lax.axis_index("node")
    first_node = device * nodes_here
    column = first_node // 4
    inverse = inverse_factor(gamma)
    node_ids = first_node + jnp.arange(nodes_here)
    keep_mask = ((node_ids < DATA_NODES - VIRTUAL) | (node_ids >= DATA_NODES)).astype(jnp.bfloat16)
    stored = groups * keep_mask[None, :, None, None, None]
    fronts = []
    for local_node in range(nodes_here):
        row_index = (first_node + local_node) % 4
        layer_grid = stored[:, local_node].reshape(stripes_here, 4, 4, 4, 4, PLANES, byte_count)
        fronts.append(
            to_front(layer_grid, row_index).reshape(
                stripes_here, 4, LAYERS // 4, PLANES, byte_count
            )
        )
    fronted = jnp.stack(fronts, axis=1)
    step_nodes = 4 // nodes_here
    received = []
    for offset in range(1, 4):
        partner_piece = from_behind(
            for_sending(
                lax.dynamic_index_in_dim(fronted, (column + offset) % 4, axis=2, keepdims=False)
            ),
            "node",
            offset * step_nodes,
        )
        received.append(((column - offset) % 4, partner_piece))
    own_front = fronted.astype(jnp.float32)
    result = own_front
    for slot_index, partner_piece in received:
        own_rows = lax.dynamic_index_in_dim(own_front, slot_index, axis=2, keepdims=False)
        theirs = partner_piece.astype(jnp.float32)
        own_lower = column < slot_index
        lower_rows = jnp.where(own_lower, own_rows, theirs)
        upper_rows = jnp.where(own_lower, theirs, own_rows)
        upper_part = mix_planes(inverse, upper_rows + mix_planes(gamma.T, lower_rows))
        values = jnp.where(own_lower, lower_rows - mix_planes(gamma, upper_part), upper_part)
        result = lax.dynamic_update_index_in_dim(result, values, slot_index, axis=2)
    backs = []
    for local_node in range(nodes_here):
        row_index = (first_node + local_node) % 4
        layer_grid = result[:, local_node].reshape(stripes_here, 4, 4, 4, 4, PLANES, byte_count)
        backs.append(
            from_front(layer_grid, row_index).reshape(stripes_here, LAYERS, PLANES, byte_count)
        )
    uncoupled = jnp.stack(backs, axis=1)
    identity = jnp.eye(PLANES, dtype=jnp.float32)
    blocks = jnp.eye(PARITY, dtype=jnp.float32)[:, :, None, None] * identity[None, None]
    weights_all = jnp.concatenate([-coeffs, blocks], axis=1)
    syndrome = jnp.einsum(
        "ijpq,sjlqb->lsipb",
        weights_all,
        lax.all_to_all(uncoupled, "node", split_axis=2, concat_axis=1, tiled=True),
        precision=precise,
    )
    energy = jnp.mean(syndrome * syndrome, axis=(3, 4))
    pool_sum = lax.psum(jnp.sum(energy, axis=1), "stripe")
    stripe_total = stripes_here * lax.axis_size("stripe")
    scores = energy / (pool_sum[:, None, :] / stripe_total + epsilon)
    return (syndrome, scores)


def solution(mesh):
    return jax.shard_map(
        local,
        mesh=mesh,
        in_specs=(P("stripe", "node", None, None, None), P(), P()),
        out_specs=(P("node", "stripe", None, None, None), P("node", "stripe", None)),
        check_vma=False,
    )
```

profile of v0, /device:TPU:0, one launch (start us, length us, event | category | flops | bytes accessed | tf_op | source)
XLA Modules:
  0.0 257.5 jit_solution(47889790480864739)
XLA Ops:
  0.8 2.5 broadcast_multiply_fusion
  3.3 2.0 copy-done.3
  7.4 3.1 %conditional.4 = (bf16[1,1,4,64,8,512]{5,4,2,3,1,0:T(8,128)(2,1)}) conditional(s32[]{:T(128)} %clamp.8, bf16[1,2,256,8,512]{4,3,2,1,0:T(8,128)(2,1)} %copy-done.3, bf16[1,2,256,8,512]{4,3,2,1,0:T(8,128)(2,1)} %copy-done.3, bf16[1,2,256,8,512]{4,3,2,1,0:T(8,128)(2,1)} %copy-done.3, ...), branch_computations={%region_0.1_spmd, %region_1.2_spmd, %region_2.3_spmd, %region_3.4_... | conditional | bytes 14680096 | solution.py:51
  7.4 3.1 %slice.130 = bf16[1,1,256,8,512]{4,3,2,1,0:T(8,128)(2,1)} slice(bf16[1,2,256,8,512]{4,3,2,1,0:T(8,128)(2,1)} %param), slice={[0:1], [0:1], [0:256], [0:8], [0:512]} | slice | bytes 4194304 | tf_op jit(solution)/shard_map/slice | solution.py:76
  10.4 6.8 %fusion.75 = (bf16[1,2,4,64,8,512]{5,4,3,2,1,0:T(8,128)(2,1)}, f32[1,2,4,64,8,512]{5,4,3,2,1,0:T(8,128)}) fusion(bf16[1,1,4,64,8,512]{5,4,2,3,1,0:T(8,128)(2,1)} %copy-done.4, bf16[1,1,4,64,8,512]{5,4,2,3,1,0:T(8,128)(2,1)} %get-tuple-element.139), kind=kLoop, calls=%fused_computation.104 | loop fusion | flops 4194304 | bytes 16777216 | tf_op jit(solution)/shard_map/stack | solution.py:82
  17.2 3.6 %dynamic-slice_bitcast_fusion = (bf16[1,2,64,8,512]{4,3,2,1,0:T(8,128)(2,1)}, bf16[1,2,64,8,512]{4,3,2,1,0:T(8,128)(2,1)}, bf16[1,2,64,8,512]{4,3,2,1,0:T(8,128)(2,1)}) fusion(bf16[1,2,4,64,8,512]{5,4,3,2,1,0:T(8,128)(2,1)} %get-tuple-element.99, s32[]{:T(128)S(6)} %select_n.139, s32[]{:T(128)S(6)} %select_n.131, s32[]{:T(128)S(6)} %select_n.122), kind=kLoop, calls=%fused_computation.54 | loop fusion | bytes 6291468 | tf_op jit(solution)/shard_map/jit(dynamic_index_in_dim)/squeeze | solution.py:88
  20.8 3.0 %collective-permute-start = (bf16[1,2,64,8,512]{4,3,2,1,0:T(8,128)(2,1)}, bf16[1,2,64,8,512]{4,3,2,1,0:T(8,128)(2,1)S(1)}, u32[]{:S(2)}, u32[]{:S(2)}) collective-permute-start(bf16[1,2,64,8,512]{4,3,2,1,0:T(8,128)(2,1)} %get-tuple-element.98), channel_id=1, source_target_pairs={{24,0},{28,4},{0,8},{4,12},{8,16},{12,20},{16,24},{20,28},{25,1},{... | collective-permute-start | bytes 3145736 | tf_op jit(solution)/shard_map/ppermute | solution.py:24
  28.0 7.6 %copy.162 = f32[1,2,4,64,8,512]{5,4,3,2,1,0:T(8,128)} copy(f32[1,2,4,64,8,512]{5,4,3,2,1,0:T(8,128)} %get-tuple-element.100) | data formatting | bytes 16777216
  38.2 22.5 %subtract_divide_fusion = (f32[1,8]{1,0:T(1,128)S(1)}, f32[1,8]{1,0:T(1,128)S(1)}, f32[1,8]{1,0:T(1,128)S(1)}, f32[1,8]{1,0:T(1,128)S(1)}, f32[1,8]{1,0:T(1,128)...) fusion(f32[8,8]{1,0:T(8,128)S(1)} %fusion.66, f32[]{:T(128)} %bitcast.83, f32[]{:T(128)} %bitcast.82, ...), kind=kLoop, calls=%fused_computation.94 | loop fusion | flops 512 | bytes 656 | tf_op jit(solution)/shard_map/div | solution.py:41
  60.9 2.1 convert_select_fusion.5
  65.0 2.2 fusion.4
  67.2 3.5 %collective-permute-done.1 = bf16[1,2,64,8,512]{4,3,2,1,0:T(8,128)(2,1)S(1)} collective-permute-done((bf16[1,2,64,8,512]{4,3,2,1,0:T(8,128)(2,1)}, bf16[1,2,64,8,512]{4,3,2,1,0:T(8,128)(2,1)S(1)}, u32[]{:S(2)}, u32[]{:S(2)}) %collective-permute-start.1) | collective-permute-done | bytes 1048608 | tf_op jit(solution)/shard_map/ppermute | solution.py:24
  70.7 2.1 fusion.30
  72.8 2.2 fusion.8
  75.1 4.0 %bitcast_dynamic-update-slice_fusion.2 = f32[1,2,4,64,8,512]{5,4,3,2,1,0:T(8,128)} fusion(f32[1,2,4,64,8,512]{5,4,3,2,1,0:T(8,128)} %copy.162, s32[]{:T(128)S(6)} %select_n.120, f32[1,2,64,8,512]{4,3,2,1,0:T(8,128)S(1)} %convert_select_fusion.5, f32[2,64,512,8]{2,3,1,0:T(8,128)S(1)} %fusion.4, pred[]{:T(512)S(6)} %lt.82, f32[8,8]{1,0:T(8,128)S(1)} %copy-done), kind=kOutput, calls=%fused_computation.32 | convolution fusion | flops 51380224 | bytes 8392709 | tf_op jit(solution)/shard_map/pq,...qb->...pb/dot_general | solution.py:28
  79.1 2.1 fusion.27
  81.3 2.2 fusion.12
  83.5 3.9 %bitcast_dynamic-update-slice_fusion.1 = f32[1,2,4,64,8,512]{5,4,3,2,1,0:T(8,128)} fusion(f32[1,2,4,64,8,512]{5,4,3,2,1,0:T(8,128)} %bitcast_dynamic-update-slice_fusion.2, s32[]{:T(128)S(6)} %select_n.129, f32[2,64,512,8]{2,3,1,0:T(8,128)S(1)} %fusion.8, bf16[1,2,64,8,512]{4,3,2,1,0:T(8,128)(2,1)S(1)} %collective-permute-done.1, ...), kind=kOutput, calls=%fused_computation.26 | convolution fusion | flops 52428800 | bytes 9441285 | tf_op jit(solution)/shard_map/pq,...qb->...pb/dot_general | solution.py:28
  87.4 3.9 %bitcast_dynamic-update-slice_fusion = f32[1,2,4,64,8,512]{5,4,3,2,1,0:T(8,128)} fusion(f32[1,2,4,64,8,512]{5,4,3,2,1,0:T(8,128)} %bitcast_dynamic-update-slice_fusion.1, s32[]{:T(128)S(6)} %select_n.137, f32[2,64,512,8]{2,3,1,0:T(8,128)S(1)} %fusion.12, bf16[1,2,64,8,512]{4,3,2,1,0:T(8,128)(2,1)S(1)} %collective-permute-done.2, ...), kind=kOutput, calls=%fused_computation.20 | convolution fusion | flops 52428800 | bytes 9441285 | tf_op jit(solution)/shard_map/pq,...qb->...pb/dot_general | solution.py:28
  91.3 5.3 %conditional.7 = (f32[1,1,256,8,512]{4,3,2,1,0:T(8,128)}) conditional(s32[]{:T(128)} %clamp.9, f32[1,2,4,64,8,512]{5,4,3,2,1,0:T(8,128)} %bitcast_dynamic-update-slice_fusion, f32[1,2,4,64,8,512]{5,4,3,2,1,0:T(8,128)} %bitcast_dynamic-update-slice_fusion, ...), branch_computations={%region_14.15_spmd, %region_15.16_spmd, %region_16.17_spmd, %regio... | conditional | bytes 16777224 | solution.py:59
  91.3 2.6 %slice.143 = f32[1,1,4,64,8,512]{5,4,3,2,1,0:T(8,128)S(1)} slice(f32[1,2,4,64,8,512]{5,4,3,2,1,0:T(8,128)} %param.13), slice={[0:1], [1:2], [0:4], [0:64], [0:8], [0:512]} | slice | bytes 8388608 | tf_op jit(solution)/shard_map/slice | solution.py:108
  94.0 2.5 copy.120
  96.7 5.2 %conditional.6 = (f32[1,1,256,8,512]{4,3,2,1,0:T(8,128)}) conditional(s32[]{:T(128)} %clamp.8, f32[1,2,4,64,8,512]{5,4,3,2,1,0:T(8,128)} %bitcast_dynamic-update-slice_fusion, f32[1,2,4,64,8,512]{5,4,3,2,1,0:T(8,128)} %bitcast_dynamic-update-slice_fusion, ...), branch_computations={%region_10.11_spmd, %region_11.12_spmd, %region_12.13_spmd, %regio... | conditional | bytes 16777224 | solution.py:59
  96.7 2.6 %slice.138 = f32[1,1,4,64,8,512]{5,4,3,2,1,0:T(8,128)S(1)} slice(f32[1,2,4,64,8,512]{5,4,3,2,1,0:T(8,128)} %param.8), slice={[0:1], [0:1], [0:4], [0:64], [0:8], [0:512]} | slice | bytes 8388608 | tf_op jit(solution)/shard_map/slice | solution.py:108
  99.3 2.6 %copy.116 = f32[1,4,4,4,4,8,512]{6,5,1,4,3,2,0:T(8,128)} copy(f32[1,4,4,4,4,8,512]{6,5,4,3,2,1,0:T(8,128)S(1)} %bitcast.307) | data formatting | bytes 8388608 | tf_op jit(solution)/shard_map/reshape;squeeze | solution.py:108
  101.9 7.9 %pad_maximum_fusion = f32[1,2,256,8,512]{4,3,1,0,2:T(8,128)} fusion(f32[1,1,256,8,512]{4,3,1,0,2:T(8,128)} %bitcast.314, f32[1,1,256,8,512]{4,3,1,0,2:T(8,128)} %bitcast.319), kind=kLoop, calls=%fused_computation | loop fusion | flops 2097152 | bytes 16777216 | tf_op jit(solution)/shard_map/stack | solution.py:112
  109.8 5.2 %all-to-all-start = ((f32[1,2,256,8,512]{4,3,1,0,2:T(8,128)}), f32[1,2,256,8,512]{4,3,1,0,2:T(8,128)}, u32[]{:S(2)}, u32[]{:S(2)}) async-start(f32[1,2,256,8,512]{4,3,1,0,2:T(8,128)} %pad_maximum_fusion), calls=%async_computation | async-start | bytes 16777216 | tf_op jit(solution)/shard_map/all_to_all | solution.py:119
  115.2 93.8 %all-to-all-done = f32[1,2,256,8,512]{4,3,1,0,2:T(8,128)} async-done(((f32[1,2,256,8,512]{4,3,1,0,2:T(8,128)}), f32[1,2,256,8,512]{4,3,1,0,2:T(8,128)}, u32[]{:S(2)}, u32[]{:S(2)}) %all-to-all-start) | async-done | bytes 8388640 | tf_op jit(solution)/shard_map/all_to_all | solution.py:119
  209.0 15.4 %copy.153 = f32[1,2,8,32,8,512]{5,1,2,4,3,0:T(2,128)} copy(f32[1,2,8,32,8,512]{5,4,1,3,2,0:T(8,128)} %bitcast.127) | data formatting | bytes 16777216 | tf_op jit(solution)/shard_map/all_to_all | solution.py:119
  224.5 10.9 %reshape.144 = f32[16,32,8,512,1]{3,0,2,1,4:T(8,128)} reshape(f32[1,8,2,32,8,512]{5,2,1,4,3,0:T(2,128)} %bitcast.303) | data formatting | bytes 16777216 | tf_op jit(solution)/shard_map/reshape.26
  235.3 8.9 %fusion.26 = (f32[32,4]{1,0:T(8,128)S(1)}, f32[32,512,4,8,1]{1,3,4,2,0:T(8,128)}) fusion(f32[4,4,8,8]{1,2,3,0:T(8,128)S(1)} %broadcast_multiply_fusion.1, f32[4,12,8,8]{1,2,3,0:T(8,128)S(1)} %copy_negate_fusion, f32[16,32,8,512,1]{3,0,2,1,4:T(8,128)} %reshape.144), kind=kOutput, calls=%fused_computation.39 | convolution fusion | flops 806358912 | bytes 10502656 | tf_op jit(solution)/shard_map/ijpq,sjlqb->lsipb/dot_general | solution.py:116
  244.3 12.1 %psum.7 = f32[32,4]{0,1:T(4,128)S(1)} all-reduce(f32[32,4]{0,1:T(4,128)S(1)} %broadcast_multiply_fusion.2), channel_id=1, replica_groups=mesh['node'=8,'stripe'=4] {'stripe'}, use_global_device_ids=true, to_apply=%region_19.20 | all-reduce | flops 128 | bytes 1024 | tf_op jit(solution)/shard_map/psum | solution.py:123
  (40 shorter events, 12.5 us)
Async XLA Ops:
  0.6 26.2 %copy-start = (f32[8,8]{1,0:T(8,128)S(1)}, f32[8,8]{1,0:T(8,128)}, u32[]{:S(2)}) copy-start(f32[8,8]{1,0:T(8,128)} %param.20) | copy-start | bytes 772
  3.3 2.0 copy-start.3
  6.0 1.3 copy-start.4
  20.8 40.1 %collective-permute-start = (bf16[1,2,64,8,512]{4,3,2,1,0:T(8,128)(2,1)}, bf16[1,2,64,8,512]{4,3,2,1,0:T(8,128)(2,1)S(1)}, u32[]{:S(2)}, u32[]{:S(2)}) collective-permute-start(bf16[1,2,64,8,512]{4,3,2,1,0:T(8,128)(2,1)} %get-tuple-element.98), channel_id=1, source_target_pairs={{24,0},{28,4},{0,8},{4,12},{8,16},{12,20},{16,24},{20,28},{25,1},{... | collective-permute-start | bytes 3145736 | tf_op jit(solution)/shard_map/ppermute | solution.py:24
  23.8 47.0 %collective-permute-start.1 = (bf16[1,2,64,8,512]{4,3,2,1,0:T(8,128)(2,1)}, bf16[1,2,64,8,512]{4,3,2,1,0:T(8,128)(2,1)S(1)}, u32[]{:S(2)}, u32[]{:S(2)}) collective-permute-start(bf16[1,2,64,8,512]{4,3,2,1,0:T(8,128)(2,1)} %get-tuple-element.97), channel_id=1, source_target_pairs={{16,0},{20,4},{24,8},{28,12},{0,16},{4,20},{8,24},{12,28},{17,1},{... | collective-permute-start | bytes 3145736 | tf_op jit(solution)/shard_map/ppermute | solution.py:24
  25.3 53.9 %collective-permute-start.2 = (bf16[1,2,64,8,512]{4,3,2,1,0:T(8,128)(2,1)}, bf16[1,2,64,8,512]{4,3,2,1,0:T(8,128)(2,1)S(1)}, u32[]{:S(2)}, u32[]{:S(2)}) collective-permute-start(bf16[1,2,64,8,512]{4,3,2,1,0:T(8,128)(2,1)} %get-tuple-element.96), channel_id=1, source_target_pairs={{8,0},{12,4},{16,8},{20,12},{24,16},{28,20},{0,24},{4,28},{9,1},{1... | collective-permute-start | bytes 3145736 | tf_op jit(solution)/shard_map/ppermute | solution.py:24
  60.9 4.1 %copy-start.2 = (f32[1,2,4,64,8,512]{5,4,3,2,1,0:T(8,128)S(1)}, f32[1,2,4,64,8,512]{5,4,3,2,1,0:T(8,128)}, u32[]{:S(2)}) copy-start(f32[1,2,4,64,8,512]{5,4,3,2,1,0:T(8,128)} %get-tuple-element.100) | copy-start | bytes 25165828
  109.8 5.3 %copy-start.5 = (f32[4,12,8,8]{1,3,2,0:T(8,128)S(1)}, f32[4,12,8,8]{1,3,2,0:T(8,128)}, u32[]{:S(2)}) copy-start(f32[4,12,8,8]{1,3,2,0:T(8,128)} %param.21) | copy-start | bytes 36868
  109.8 99.2 %all-to-all-start = ((f32[1,2,256,8,512]{4,3,1,0,2:T(8,128)}), f32[1,2,256,8,512]{4,3,1,0,2:T(8,128)}, u32[]{:S(2)}, u32[]{:S(2)}) async-start(f32[1,2,256,8,512]{4,3,1,0,2:T(8,128)} %pad_maximum_fusion), calls=%async_computation | async-start | bytes 16777216 | tf_op jit(solution)/shard_map/all_to_all | solution.py:119
  235.3 21.7 %copy-start.1 = (f32[8,8]{1,0:T(8,128)S(1)}, f32[8,8]{1,0:T(8,128)}, u32[]{:S(2)}) copy-start(f32[8,8]{1,0:T(8,128)} %param.20) | copy-start | bytes 772
where the time goes:
time: 262 us; the launch traced here: 257 us
  waiting for transfers between devices  97.3 us (37%)
  local copies, waits for them, and re-layouts  56.5 us (22%)
  other arithmetic  44.5 us (17%)
  matrix products  34 us (13%)
  blocking collectives  12.1 us (5%)
  starting transfers between devices  11.2 us (4%)
    all_to_all x1, waiting for transfers between devices, local(): lax.all_to_all(uncoupled, 'node', split_axis=2, concat_axis=1, tiled=True)  93.8 us
    dot_general x9, matrix products, mix_planes(): return jnp.einsum('pq,...qb->...pb', matrix, values, precision=precise)  24.7 us
    div x1, other arithmetic, inverse_factor(): solved_rows.append(running / factor[row_at, row_at])  22.5 us
    all_to_all x1, local copies, waits for them, and re-layouts, local(): lax.all_to_all(uncoupled, 'node', split_axis=2, concat_axis=1, tiled=True)  15.4 us
    psum x1, blocking collectives, local(): pool_sum = lax.psum(jnp.sum(energy, axis=1), 'stripe')  12.1 us
    unnamed x13, local copies, waits for them, and re-layouts  11 us
    another operation x1, local copies, waits for them, and re-layouts  10.9 us
    dot_general x1, matrix products, local(): jnp.einsum('ijpq,sjlqb->lsipb', weights_all, lax.all_to_all(uncoupled, 'n...  8.93 us
  transfers between devices with their start and end apart: 4, of which 2 were waited for; matrix products, arithmetic and copies ran while one was open for 19% of the time, Pallas kernels for 0%

commit v1 on v0

v1 whole, which is shorter than its diff:
```python
import jax
import jax.numpy as jnp
from jax import lax
from jax.experimental import pallas as pl
from jax.experimental.pallas import tpu as pltpu
from jax.sharding import PartitionSpec as P


PLANES = 8
PARITY = 4
DATA_NODES = 12
VIRTUAL = 2
OUT_ROWS = PARITY * PLANES
PARTS = 3


precise = lax.Precision.HIGHEST
epsilon = 1e-06
WIDTH = PARTS * 4 * PLANES
MIB = 1024 * 1024


def dot32(a, b):
    return jnp.dot(a, b, precision=precise)


def inverse_of(matrix):
    size = matrix.shape[0]
    row_ids = lax.broadcasted_iota(jnp.int32, (size, size), 0)
    left = matrix
    right = (row_ids == lax.broadcasted_iota(jnp.int32, (size, size), 1)).astype(jnp.float32)
    for at in range(size):
        scale = 1.0 / left[at : at + 1, at : at + 1]
        left_row = left[at : at + 1] * scale
        right_row = right[at : at + 1] * scale
        factor = left[:, at : at + 1]
        here = row_ids == at
        left = jnp.where(here, left_row, left - factor * left_row)
        right = jnp.where(here, right_row, right - factor * right_row)
    return 0.5 * (right + right.T)


def table_kernel(place_ref, gamma_ref, gamma_t_ref, encode_ref, lines_ref, extra_ref):
    column = place_ref[0]
    gamma, gamma_t = gamma_ref[...], gamma_t_ref[...]
    eye_rows = lax.broadcasted_iota(jnp.int32, (PLANES, PLANES), 0)
    eye_lanes = lax.broadcasted_iota(jnp.int32, (PLANES, PLANES), 1)
    identity = (eye_rows == eye_lanes).astype(jnp.float32)
    inverse = inverse_of(identity + dot32(gamma_t, gamma))
    gain = dot32(gamma, inverse)
    wide_rows = lax.broadcasted_iota(jnp.int32, (PLANES, WIDTH), 0)
    wide_lanes = lax.broadcasted_iota(jnp.int32, (PLANES, WIDTH), 1)
    spread = (wide_rows == wide_lanes % PLANES).astype(jnp.float32)

    def tiled(matrix):
        return jnp.concatenate([dot32(matrix, spread)] * 4, axis=0)

    plain = jnp.concatenate([spread] * 4, axis=0)
    lower = tiled(identity - dot32(gain, gamma_t))
    upper = tiled(inverse)
    from_upper = tiled(-gain)
    from_lower = tiled(dot32(inverse, gamma_t))
    block_in = lax.broadcasted_iota(jnp.int32, (4 * PLANES, WIDTH), 0) // PLANES
    lanes = lax.broadcasted_iota(jnp.int32, (4 * PLANES, WIDTH), 1)
    block_out = (lanes // PLANES) % 4
    zero = jnp.zeros((4 * PLANES, WIDTH), jnp.float32)

    def parts(product):
        part = lax.broadcasted_iota(jnp.int32, product.shape, 1) // (4 * PLANES)
        head = product.astype(jnp.bfloat16).astype(jnp.float32)
        rest = product - head
        middle = rest.astype(jnp.bfloat16).astype(jnp.float32)
        tail = rest - middle
        chosen = jnp.where(part == 0, head, jnp.where(part == 1, middle, tail))
        return chosen.astype(jnp.bfloat16)

    def real(source, row):
        node = 4 * source + row
        return jnp.where((node < DATA_NODES - VIRTUAL) | (node >= DATA_NODES), 1.0, 0.0)

    upto3 = jnp.concatenate([encode_ref[row] for row in range(3)], axis=0)
    for o in range(4):
        source = column ^ o

        def own(digit):
            return jnp.where(source == digit, plain, jnp.where(source < digit, lower, upper))

        coupled = jnp.where(block_out < source, from_upper, from_lower)
        coupled = jnp.where((block_in == block_out) & (block_in != source), coupled, zero)
        for j in range(4):
            from_own = (block_in == source) & (block_out == j)
            step = jnp.where(from_own, own(j), jnp.where(source == j, coupled, zero))
            product = dot32(upto3, step)
            for row in range(3):
                piece = product[row * OUT_ROWS : (row + 1) * OUT_ROWS] * real(source, row)
                lines_ref[row, o, j * OUT_ROWS : (j + 1) * OUT_ROWS] = parts(piece)
            piece = dot32(encode_ref[3], jnp.where(from_own, own(column), zero))
            piece = piece * real(source, 3)
            lines_ref[3, o, j * OUT_ROWS : (j + 1) * OUT_ROWS] = parts(piece)
    away = jnp.where(block_in < column, from_upper, from_lower)
    away = jnp.where((block_in == (column ^ block_out)) & (block_out != 0), away, zero)
    extra_ref[...] = parts(dot32(encode_ref[3], away) * real(column, 3))


def build_tables(place, gamma, coeffs):
    by_column = coeffs.reshape(PARITY, 3, 4, PLANES, PLANES)
    data_part = -jnp.transpose(by_column, (2, 0, 3, 1, 4)).reshape(4, OUT_ROWS, 3 * PLANES)
    own_parity = jnp.arange(OUT_ROWS)[None, :] - PLANES * jnp.arange(4)[:, None]
    parity_part = (own_parity[:, :, None] == jnp.arange(PLANES)).astype(jnp.float32)
    encode = jnp.concatenate([data_part, parity_part], axis=-1)
    vmem = pl.BlockSpec(memory_space=pltpu.VMEM)
    return pl.pallas_call(
        table_kernel,
        out_shape=(
            jax.ShapeDtypeStruct((4, 4, 4 * OUT_ROWS, WIDTH), jnp.bfloat16),
            jax.ShapeDtypeStruct((OUT_ROWS, WIDTH), jnp.bfloat16),
        ),
        in_specs=[pl.BlockSpec(memory_space=pltpu.SMEM), vmem, vmem, vmem],
        out_specs=(vmem, vmem),
        compiler_params=pltpu.CompilerParams(vmem_limit_bytes=16 * MIB),
        name="tables",
        cost_estimate=pl.CostEstimate(flops=1_000_000_000, bytes_accessed=MIB, transcendentals=0),
    )(place, gamma, gamma.T, encode)


def gathered(slabs):
    block = jnp.concatenate([slab.astype(jnp.float32) for slab in slabs], axis=0)
    block = block.astype(jnp.bfloat16)
    return jnp.concatenate([block] * PARTS, axis=0)


def line_at(number, row):
    shift = 2 * jnp.minimum(row, 2)
    base = ((number >> shift) << (shift + 2)) | (number & ((1 << shift) - 1))
    return [base + (at << shift) for at in range(4)]


def mixed(matrix, slabs):
    return jnp.dot(matrix, gathered(slabs), preferred_element_type=jnp.float32)


def own_kernel(layers_here, place_ref, own_ref, lines_ref, extra_ref, out_ref):
    nodes_here = own_ref.shape[1]
    column_layers = out_ref.shape[0]
    column, peer = place_ref[0], place_ref[1]
    flip = peer * layers_here
    for local in range(nodes_here):
        row = peer * nodes_here + local

        def body(number, carry):
            line = line_at(number, row)
            total = mixed(
                lines_ref[row, 0],
                [own_ref[0, local, column * column_layers + layer] for layer in line],
            )
            for at, layer in enumerate(line):
                value = total[at * OUT_ROWS : (at + 1) * OUT_ROWS]
                spot = layer ^ flip
                out_ref[spot] = value if local == 0 else out_ref[spot] + value
            return carry

        lax.fori_loop(0, column_layers // 4, body, 0, unroll=2)

    @pl.when((peer + 1) * nodes_here == 4)
    def _():
        def body(layer, carry):
            away = [
                own_ref[0, nodes_here - 1, (column ^ o) * column_layers + layer] for o in range(4)
            ]
            out_ref[layer ^ flip] += mixed(extra_ref[...], away)
            return carry

        lax.fori_loop(0, column_layers, body, 0, unroll=4)


def add_rows(layers_here, nodes_here, place_ref, lines_ref, pieces, before_ref, total_ref):
    peer = place_ref[1]
    flip = peer * layers_here
    for order, (local, sources) in enumerate(pieces.items()):
        row = peer * nodes_here + local

        def body(number, carry):
            line = line_at(number, row)
            total = None
            for offset, ref in sources:
                term = mixed(lines_ref[row, offset], [ref[0, 0, layer] for layer in line])
                total = term if total is None else total + term
            for at, layer in enumerate(line):
                spot = layer ^ flip
                start = before_ref[spot] if order == 0 else total_ref[spot]
                total_ref[spot] = start + total[at * OUT_ROWS : (at + 1) * OUT_ROWS]
            return carry

        lax.fori_loop(0, total_ref.shape[0] // 4, body, 0, unroll=2)


def across_kernel(layers_here, nodes_here, place_ref, lines_ref, before_ref, far_ref, total_ref):
    pieces = {at: [(3, far_ref.at[:, pl.ds(at, 1)])] for at in range(nodes_here)}
    add_rows(layers_here, nodes_here, place_ref, lines_ref, pieces, before_ref, total_ref)


def beside_kernel(layers_here, nodes_here, rows, place_ref, lines_ref, before_ref, *refs):
    piece_refs, out_refs, total_ref = refs[: 2 * rows], refs[2 * rows : -1], refs[-1]
    pieces = {at: [(1, piece_refs[2 * at]), (2, piece_refs[2 * at + 1])] for at in range(rows)}
    add_rows(layers_here, nodes_here, place_ref, lines_ref, pieces, before_ref, total_ref)
    for slot in reversed(range(len(out_refs))):

        def copy(at, carry):
            out_refs[slot][at] = total_ref[slot * layers_here + at]
            return carry

        lax.fori_loop(0, layers_here, copy, 0, unroll=4)


def finish_kernel(nodes_here, place_ref, lines_ref, before_ref, *refs):
    piece_refs, refs = refs[:-5], refs[-5:]
    out_ref, energy_ref, value_ref, lanes_ref, sems = refs
    layers_here, _, byte_count = value_ref.shape
    peer = place_ref[1]
    copies = []
    for first in range(0, layers_here, 16):
        for number in range(4):
            line = [first + number + 4 * at for at in range(4)]
            total = None
            for order, ref in enumerate(piece_refs):
                row = (peer ^ (order // 2)) * nodes_here + nodes_here - 1
                term = mixed(lines_ref[row, 1 + order % 2], [ref[0, 0, layer] for layer in line])
                total = term if total is None else total + term
            for at, layer in enumerate(line):
                value = before_ref[layer]
                if total is not None:
                    value = value + total[at * OUT_ROWS : (at + 1) * OUT_ROWS]
                value_ref[layer] = value
                square = value * value
                lanes = sum(square[:, i * 128 : (i + 1) * 128] for i in range(byte_count // 128))
                for i in range(PARITY):
                    lanes_ref[i, layer : layer + 1] = jnp.sum(
                        lanes[i * PLANES : (i + 1) * PLANES], axis=0, keepdims=True
                    )
        rows = pl.ds(first, 16)
        copy = pltpu.make_async_copy(value_ref.at[rows], out_ref.at[rows], sems.at[first // 16])
        copy.start()
        copies.append(copy)
    sums = [jnp.sum(lanes_ref[i], axis=1, keepdims=True) for i in range(PARITY)]
    energy_ref[...] = jnp.concatenate(sums, axis=1) * (1.0 / (PLANES * byte_count))
    for copy in copies:
        copy.wait()


def kernel_call(body, out_shape, operands, mflops, mib, out_specs=None, scratch=()):
    smem = pl.BlockSpec(memory_space=pltpu.SMEM)
    vmem = pl.BlockSpec(memory_space=pltpu.VMEM)
    if out_specs is None:
        out_specs = jax.tree.map(lambda _: vmem, out_shape)
    return pl.pallas_call(
        body,
        out_shape=out_shape,
        in_specs=[smem] + [vmem] * (len(operands) - 1),
        out_specs=out_specs,
        scratch_shapes=scratch,
        compiler_params=pltpu.CompilerParams(vmem_limit_bytes=24 * MIB),
        cost_estimate=pl.CostEstimate(
            flops=mflops * 1_000_000, bytes_accessed=mib * MIB, transcendentals=0
        ),
    )(*operands)


def scrub(groups, gamma, coeffs):
    stripes_here, nodes_here, layers, planes, byte_count = groups.shape
    devices = lax.axis_size("node")
    peers = devices // 4
    layers_here = layers // devices
    column_layers = layers // 4
    device = lax.axis_index("node")
    column, peer = device // peers, device % peers
    place = jnp.stack([column, peer]).astype(jnp.int32)
    direct = nodes_here == 2
    rows = nodes_here - 1 if direct else nodes_here

    def cut(source, first_row, row_count, offset, slot=None):
        first, count = (column ^ offset) * column_layers, column_layers
        if slot is not None:
            first, count = first + (peer ^ slot) * layers_here, layers_here
        return lax.dynamic_slice(
            source,
            (0, first_row, first, 0, 0),
            (stripes_here, row_count, count, planes, byte_count),
        )

    def send(piece, offset, slot=0):
        route = [(i, (((i // peers) ^ offset) * peers + i % peers) ^ slot) for i in range(devices)]
        return lax.ppermute(piece, "node", route)

    across_piece = cut(groups, 0, nodes_here, 3)
    source, across_piece = lax.optimization_barrier((groups, across_piece))
    across_piece = send(across_piece, 3)
    plan = [(at, 1, offset, None) for at in range(rows) for offset in (1, 2)]
    if direct:
        plan += [(rows, 1, offset, slot) for slot in range(peers) for offset in (1, 2)]
    cuts = [cut(source, *entry) for entry in plan]
    cuts = lax.optimization_barrier(tuple(cuts))
    arrived = [send(piece, entry[2], entry[3] or 0) for piece, entry in zip(cuts, plan)]
    beside_pieces, last_pieces = arrived[: 2 * rows], arrived[2 * rows :]
    lines, extra = build_tables(place, gamma, coeffs)

    all_layers = jax.ShapeDtypeStruct((column_layers, OUT_ROWS, byte_count), jnp.float32)
    part = jax.ShapeDtypeStruct((layers_here, OUT_ROWS, byte_count), jnp.float32)
    own = kernel_call(
        lambda *refs: own_kernel(layers_here, *refs),
        all_layers,
        (place, groups, lines, extra),
        2000,
        8,
    )
    across = kernel_call(
        lambda *refs: across_kernel(layers_here, nodes_here, *refs),
        all_layers,
        (place, lines, own, across_piece),
        2000,
        9,
    )
    sums = kernel_call(
        lambda *refs: beside_kernel(layers_here, nodes_here, rows, *refs),
        [part] * peers,
        (place, lines, across, *beside_pieces),
        2000,
        9,
        scratch=[pltpu.VMEM(all_layers.shape, jnp.float32)],
    )
    total = sums[0]
    for slot in range(1, peers):
        route = [(i, (i // peers) * peers + ((i % peers) ^ slot)) for i in range(devices)]
        total = total + lax.ppermute(sums[slot], "node", route)

    syndrome, energy = kernel_call(
        lambda *refs: finish_kernel(nodes_here, *refs),
        (part, jax.ShapeDtypeStruct((layers_here, PARITY), jnp.float32)),
        (place, lines, total, *last_pieces),
        500,
        4,
        out_specs=(
            pl.BlockSpec(memory_space=pl.ANY),
            pl.BlockSpec(memory_space=pltpu.VMEM),
        ),
        scratch=[
            pltpu.VMEM(part.shape, jnp.float32),
            pltpu.VMEM((PARITY, layers_here, 128), jnp.float32),
            pltpu.SemaphoreType.DMA((layers_here // 16,)),
        ],
    )
    stripes = lax.axis_size("stripe")
    pool = energy
    if stripes & (stripes - 1) == 0:
        distance = 1
        while distance < stripes:
            pool = pool + lax.ppermute(
                pool, "stripe", [(i, i ^ distance) for i in range(stripes)]
            )
            distance *= 2
    else:
        pool = lax.psum(energy, "stripe")
    scores = energy / (pool / (stripes * stripes_here) + epsilon)
    return (
        syndrome.reshape(layers_here, stripes_here, PARITY, planes, byte_count),
        scores.reshape(layers_here, stripes_here, PARITY),
    )


def solution(mesh):
    return jax.shard_map(
        scrub,
        mesh=mesh,
        in_specs=(P("stripe", "node", None, None, None), P(), P()),
        out_specs=(P("node", "stripe", None, None, None), P("node", "stripe", None)),
        check_vma=False,
    )
```

time: 262 us -> 70.8 us (0.27); the launches traced: 257 us -> 70.6 us
  waiting for transfers between devices: 97.3 us -> 30 us
  local copies, waits for them, and re-layouts: 56.5 us -> 9.24 us
  other arithmetic: 44.5 us -> 0.84 us
  matrix products: 34 us -> 0 us
  Pallas kernels: 0 us -> 17 us
  blocking collectives: 12.1 us -> 0 us
    all_to_all x1 -> x0, waiting for transfers between devices: 93.8 us -> none  [local(): lax.all_to_all(uncoupled, 'node', split_axis=2, concat_axis=1, tiled=True)]
    dot_general x12 -> x0, matrix products: 34 us -> none  [the longest x9 24.7 us: mix_planes(): return jnp.einsum('pq,...qb->...pb', matrix, values, precision=precise)]
    ppermute x3 -> x10, waiting for transfers between devices: 3.5 us -> 30 us  [the longest x7 25.5 us: send(): return lax.ppermute(piece, 'node', route)]
    div x4 -> x1, other arithmetic: 23.1 us -> 0.01 us  [scrub(): scores = energy / (pool / (stripes * stripes_here) + epsilon)]
    pallas_call x0 -> x5, Pallas kernels: none -> 17 us  [the longest x4 13.9 us: kernel_call(): pl.pallas_call(body, out_shape=out_shape, in_specs=[smem] + [vmem] * (len...]
    another operation x5 -> x0, local copies, waits for them, and re-layouts: 16.2 us -> none
    another operation x5 -> x1, other arithmetic: 16 us -> 0.08 us  [scrub(): place = jnp.stack([column, peer]).astype(jnp.int32)]
    all_to_all x1 -> x0, local copies, waits for them, and re-layouts: 15.4 us -> none  [local(): lax.all_to_all(uncoupled, 'node', split_axis=2, concat_axis=1, tiled=True)]
  transfers between devices with their start and end apart: 4 -> 10, of which waited for: 2 -> 9; matrix products, arithmetic and copies ran while one was open for 19% -> 8% of each run, Pallas kernels for 0% -> 16%
where the time goes in v1:
time: 70.8 us; the launch traced here: 70.6 us
  waiting for transfers between devices  30 us (42%)
  Pallas kernels  17 us (24%)
  starting transfers between devices  12.7 us (18%)
  local copies, waits for them, and re-layouts  9.24 us (13%)
  other arithmetic  0.84 us (1%)
  between operations  0.82 us (1%)
    ppermute x7, waiting for transfers between devices, send(): return lax.ppermute(piece, 'node', route)  25.5 us
    pallas_call x4, Pallas kernels, kernel_call(): pl.pallas_call(body, out_shape=out_shape, in_specs=[smem] + [vmem] * (len...  13.9 us
    ppermute x7, starting transfers between devices, send(): return lax.ppermute(piece, 'node', route)  8.45 us
    dynamic_slice x3, local copies, waits for them, and re-layouts, cut(): lax.dynamic_slice(source, (0, first_row, first, 0, 0), (stripes_here, row...  5.77 us
    ppermute x2, starting transfers between devices, scrub(): lax.ppermute(pool, 'stripe', [(i, i ^ distance) for i in range(stripes)])  4.22 us
    ppermute x2, waiting for transfers between devices, scrub(): lax.ppermute(pool, 'stripe', [(i, i ^ distance) for i in range(stripes)])  4.22 us
    pallas_call x1, Pallas kernels, build_tables(): pl.pallas_call(table_kernel, out_shape=(jax.ShapeDtypeStruct((4, 4, 4 * O...  3.04 us
    unnamed x16, local copies, waits for them, and re-layouts  2.54 us
  transfers between devices with their start and end apart: 10, of which 9 were waited for; matrix products, arithmetic and copies ran while one was open for 8% of the time, Pallas kernels for 16%

profile of v1, /device:TPU:0, one launch (start us, length us, event | category | flops | bytes accessed | tf_op | source)
XLA Modules:
  0.0 70.6 jit_solution(12776968891922190480)
XLA Ops:
  0.7 1.3 %constant_dynamic-slice_fusion.6 = bf16[1,2,64,8,512]{4,3,2,1,0:T(8,128)(2,1)S(1)} fusion(bf16[1,2,256,8,512]{4,3,2,1,0:T(8,128)(2,1)} %refs_1_.1, s32[]{:T(128)S(6)} %select_n.34), kind=kLoop, calls=%fused_computation.11 | loop fusion | bytes 2097156 | tf_op jit(solution)/shard_map/dynamic_slice | solution.py:284
  2.0 4.0 %collective-permute-start = (bf16[1,2,64,8,512]{4,3,2,1,0:T(8,128)(2,1)S(1)}, bf16[1,2,64,8,512]{4,3,2,1,0:T(8,128)(2,1)S(1)}, u32[]{:S(2)}, u32[]{:S(2)}) collective-permute-start(bf16[1,2,64,8,512]{4,3,2,1,0:T(8,128)(2,1)S(1)} %constant_dynamic-slice_fusion.6), channel_id=1, source_target_pairs={{0,24},{4,28},{8,16},{12,20},{16,8},{20,12},{24,0},{28,4},{1,25},{... | collective-permute-start | bytes 3145736 | tf_op jit(solution)/shard_map/ppermute | solution.py:292
  6.0 2.2 %constant_dynamic-slice_fusion.4 = (bf16[1,1,64,8,512]{4,3,2,1,0:T(8,128)(2,1)}, bf16[1,1,64,8,512]{4,3,2,1,0:T(8,128)(2,1)}) fusion(bf16[1,2,256,8,512]{4,3,2,1,0:T(8,128)(2,1)} %refs_1_.1, s32[]{:T(128)S(6)} %select_n.36, s32[]{:T(128)S(6)} %select_n.35), kind=kLoop, calls=%fused_computation.9 | loop fusion | bytes 2097160 | tf_op jit(solution)/shard_map/dynamic_slice | solution.py:284
  8.2 2.2 %constant_dynamic-slice_fusion = (bf16[1,1,32,8,512]{4,3,2,1,0:T(8,128)(2,1)}, bf16[1,1,32,8,512]{4,3,2,1,0:T(8,128)(2,1)}, bf16[1,1,32,8,512]{4,3,2,1,0:T(8,128)(2,1)}, bf16[1,1,32,8,512]{4,3,2,1,0:T(8,128)(2,1)}) fusion(bf16[1,2,256,8,512]{4,3,2,1,0:T(8,128)(2,1)} %refs_1_.1, s32[]{:T(128)S(6)} %select_n.40, s32[]{:T(128)S(6)} %select_n.39, ...), kind=kLoop, calls=%fused_computation.5 | loop fusion | bytes 2097168 | tf_op jit(solution)/shard_map/dynamic_slice | solution.py:284
  10.4 0.5 collective-permute-start.1
  11.0 0.1 collective-permute-start.2
  11.1 0.3 copy.10
  11.4 0.1 copy.15
  11.5 0.1 reshape.41
  11.7 0.1 fusion
  12.1 3.0 %tables.1 = (bf16[4,4,128,96]{3,2,1,0:T(8,128)(2,1)S(1)}, bf16[32,96]{1,0:T(8,128)(2,1)S(1)}) custom-call(s32[2]{0:T(128)S(1)} %pad_add_fusion.place_ref.refs_0_, f32[8,8]{1,0:T(8,128)S(1)} %copy-done.1, f32[8,8]{1,0:T(8,128)S(1)} %bitcast.10, f32[4,32,32]{2,1,0:T(8,128)S(1)} %pad_maximum_fusion.encode_ref), custom_call_target="tpu_custom_call" | custom-call | flops 1000000000 | bytes 1048576 | tf_op jit(solution)/shard_map/tables/pallas_call | solution.py:112
  15.1 2.2 %copy-done = bf16[1,2,256,8,512]{4,3,2,1,0:T(8,128)(2,1)S(1)} copy-done((bf16[1,2,256,8,512]{4,3,2,1,0:T(8,128)(2,1)S(1)}, bf16[1,2,256,8,512]{4,3,2,1,0:T(8,128)(2,1)}, u32[]{:S(2)}) %copy-start) | copy-done | bytes 4194328
  17.3 4.0 %shard_map.50.refs_2_ = f32[64,32,512]{2,1,0:T(8,128)S(1)} custom-call(s32[2]{0:T(128)S(1)} %pad_add_fusion.place_ref.refs_0_, bf16[1,2,256,8,512]{4,3,2,1,0:T(8,128)(2,1)S(1)} %copy-done, bf16[4,4,128,96]{3,2,1,0:T(8,128)(2,1)S(1)} %get-tuple-element.16.refs_2_.refs_1_, bf16[32,96]{1,0:T(8,128)(2,1)S(1)} %get-tuple-element.17.refs_3_), custom_call_target="tpu_custom_call" | custom-call | flops 2000000000 | bytes 8388608 | tf_op jit(solution)/shard_map/pallas_call | solution.py:255
  21.3 8.8 %collective-permute-done.refs_3_ = bf16[1,2,64,8,512]{4,3,2,1,0:T(8,128)(2,1)S(1)} collective-permute-done((bf16[1,2,64,8,512]{4,3,2,1,0:T(8,128)(2,1)S(1)}, bf16[1,2,64,8,512]{4,3,2,1,0:T(8,128)(2,1)S(1)}, u32[]{:S(2)}, u32[]{:S(2)}) %collective-permute-start) | collective-permute-done | bytes 1048608 | tf_op jit(solution)/shard_map/ppermute | solution.py:292
  30.0 4.0 %shard_map.51.refs_2_ = f32[64,32,512]{2,1,0:T(8,128)S(1)} custom-call(s32[2]{0:T(128)S(1)} %pad_add_fusion.place_ref.refs_0_, bf16[4,4,128,96]{3,2,1,0:T(8,128)(2,1)S(1)} %get-tuple-element.16.refs_2_.refs_1_, f32[64,32,512]{2,1,0:T(8,128)S(1)} %shard_map.50.refs_2_, bf16[1,2,64,8,512]{4,3,2,1,0:T(8,128)(2,1)S(1)} %collective-permute-done.refs_3_), custom_call_target="tpu_custom_call" | custom-call | flops 2000000000 | bytes 9437184 | tf_op jit(solution)/shard_map/pallas_call | solution.py:255
  34.1 6.6 %collective-permute-done.1.refs_3_ = bf16[1,1,64,8,512]{4,3,2,1,0:T(8,128)(2,1)S(1)} collective-permute-done((bf16[1,1,64,8,512]{4,3,2,1,0:T(8,128)(2,1)}, bf16[1,1,64,8,512]{4,3,2,1,0:T(8,128)(2,1)S(1)}, u32[]{:S(2)}, u32[]{:S(2)}) %collective-permute-start.1) | collective-permute-done | bytes 524320 | tf_op jit(solution)/shard_map/ppermute | solution.py:292
  40.7 3.2 %shard_map.52 = (f32[32,32,512]{2,1,0:T(8,128)S(1)}, f32[32,32,512]{2,1,0:T(8,128)S(1)}) custom-call(s32[2]{0:T(128)S(1)} %pad_add_fusion.place_ref.refs_0_, bf16[4,4,128,96]{3,2,1,0:T(8,128)(2,1)S(1)} %get-tuple-element.16.refs_2_.refs_1_, f32[64,32,512]{2,1,0:T(8,128)S(1)} %shard_map.51.refs_2_, ...), custom_call_target="tpu_custom_call" | custom-call | flops 2000000000 | bytes 9437184 | tf_op jit(solution)/shard_map/pallas_call | solution.py:255
  43.9 1.6 %collective-permute-start.4 = (bf16[1,1,32,8,512]{4,3,2,1,0:T(8,128)(2,1)S(1)}, bf16[1,1,32,8,512]{4,3,2,1,0:T(8,128)(2,1)S(1)}, u32[]{:S(2)}, u32[]{:S(2)}) collective-permute-start(bf16[1,1,32,8,512]{4,3,2,1,0:T(8,128)(2,1)S(1)} %copy-done.5), channel_id=1, source_target_pairs={{0,8},{4,12},{8,0},{12,4},{16,24},{20,28},{24,16},{28,20},{1,9},{5... | collective-permute-start | bytes 786440 | tf_op jit(solution)/shard_map/ppermute | solution.py:292
  45.5 1.4 %collective-permute-start.5 = (bf16[1,1,32,8,512]{4,3,2,1,0:T(8,128)(2,1)S(1)}, bf16[1,1,32,8,512]{4,3,2,1,0:T(8,128)(2,1)S(1)}, u32[]{:S(2)}, u32[]{:S(2)}) collective-permute-start(bf16[1,1,32,8,512]{4,3,2,1,0:T(8,128)(2,1)S(1)} %copy-done.4), channel_id=1, source_target_pairs={{0,16},{4,20},{8,24},{12,28},{16,0},{20,4},{24,8},{28,12},{1,17},{... | collective-permute-start | bytes 786440 | tf_op jit(solution)/shard_map/ppermute | solution.py:292
  46.9 0.9 %collective-permute-start.7 = (bf16[1,1,32,8,512]{4,3,2,1,0:T(8,128)(2,1)S(1)}, bf16[1,1,32,8,512]{4,3,2,1,0:T(8,128)(2,1)S(1)}, u32[]{:S(2)}, u32[]{:S(2)}) collective-permute-start(bf16[1,1,32,8,512]{4,3,2,1,0:T(8,128)(2,1)S(1)} %copy-done.2), channel_id=1, source_target_pairs={{0,20},{4,16},{8,28},{12,24},{16,4},{20,0},{24,12},{28,8},{1,21},{... | collective-permute-start | bytes 786440 | tf_op jit(solution)/shard_map/ppermute | solution.py:292
  47.8 0.3 collective-permute-done.3
  48.1 0.5 add.65.refs_2_
  48.6 4.6 %collective-permute-done.4.refs_3_ = bf16[1,1,32,8,512]{4,3,2,1,0:T(8,128)(2,1)S(1)} collective-permute-done((bf16[1,1,32,8,512]{4,3,2,1,0:T(8,128)(2,1)S(1)}, bf16[1,1,32,8,512]{4,3,2,1,0:T(8,128)(2,1)S(1)}, u32[]{:S(2)}, u32[]{:S(2)}) %collective-permute-start.4) | collective-permute-done | bytes 262176 | tf_op jit(solution)/shard_map/ppermute | solution.py:292
  53.2 1.5 %collective-permute-done.5.refs_4_ = bf16[1,1,32,8,512]{4,3,2,1,0:T(8,128)(2,1)S(1)} collective-permute-done((bf16[1,1,32,8,512]{4,3,2,1,0:T(8,128)(2,1)S(1)}, bf16[1,1,32,8,512]{4,3,2,1,0:T(8,128)(2,1)S(1)}, u32[]{:S(2)}, u32[]{:S(2)}) %collective-permute-start.5) | collective-permute-done | bytes 262176 | tf_op jit(solution)/shard_map/ppermute | solution.py:292
  54.7 3.0 %collective-permute-done.6.refs_5_ = bf16[1,1,32,8,512]{4,3,2,1,0:T(8,128)(2,1)S(1)} collective-permute-done((bf16[1,1,32,8,512]{4,3,2,1,0:T(8,128)(2,1)S(1)}, bf16[1,1,32,8,512]{4,3,2,1,0:T(8,128)(2,1)S(1)}, u32[]{:S(2)}, u32[]{:S(2)}) %collective-permute-start.6) | collective-permute-done | bytes 262176 | tf_op jit(solution)/shard_map/ppermute | solution.py:292
  57.7 0.9 %collective-permute-done.7.refs_6_ = bf16[1,1,32,8,512]{4,3,2,1,0:T(8,128)(2,1)S(1)} collective-permute-done((bf16[1,1,32,8,512]{4,3,2,1,0:T(8,128)(2,1)S(1)}, bf16[1,1,32,8,512]{4,3,2,1,0:T(8,128)(2,1)S(1)}, u32[]{:S(2)}, u32[]{:S(2)}) %collective-permute-start.7) | collective-permute-done | bytes 262176 | tf_op jit(solution)/shard_map/ppermute | solution.py:292
  58.6 2.8 %shard_map.53 = (f32[32,32,512]{2,1,0:T(8,128)}, f32[32,4]{1,0:T(8,128)S(1)}) custom-call(s32[2]{0:T(128)S(1)} %pad_add_fusion.place_ref.refs_0_, bf16[4,4,128,96]{3,2,1,0:T(8,128)(2,1)S(1)} %get-tuple-element.16.refs_2_.refs_1_, f32[32,32,512]{2,1,0:T(8,128)S(1)} %add.65.refs_2_, bf16[1,1,32,8,512]{4,3,2,1,0:T(8,128)(2,1)S(1)} %collective-permute-done.4.refs_3_, ...), custom_call_target="tpu_custom_call" | custom-call | flops 500000000 | bytes 4194304 | tf_op jit(solution)/shard_map/pallas_call | solution.py:255
  61.5 1.6 %collective-permute-start.8 = (f32[32,4]{1,0:T(8,128)S(1)}, f32[32,4]{1,0:T(8,128)S(1)}, u32[]{:S(2)}, u32[]{:S(2)}) collective-permute-start(f32[32,4]{1,0:T(8,128)S(1)} %get-tuple-element.29), channel_id=1, source_target_pairs={{0,1},{1,0},{2,3},{3,2},{4,5},{5,4},{6,7},{7,6},{8,9},{9,8},{10,11... | collective-permute-start | bytes 1544 | tf_op jit(solution)/shard_map/ppermute | solution.py:356
  63.1 2.2 %collective-permute-done.8 = f32[32,4]{1,0:T(8,128)S(1)} collective-permute-done((f32[32,4]{1,0:T(8,128)S(1)}, f32[32,4]{1,0:T(8,128)S(1)}, u32[]{:S(2)}, u32[]{:S(2)}) %collective-permute-start.8) | collective-permute-done | bytes 544 | tf_op jit(solution)/shard_map/ppermute | solution.py:356
  65.3 2.6 %collective-permute-start.9 = (f32[32,4]{1,0:T(8,128)S(1)}, f32[32,4]{1,0:T(8,128)S(1)}, u32[]{:S(2)}, u32[]{:S(2)}) collective-permute-start(f32[32,4]{1,0:T(8,128)S(1)} %add.66), channel_id=1, source_target_pairs={{0,2},{1,3},{2,0},{3,1},{4,6},{5,7},{6,4},{7,5},{8,10},{9,11},{10,... | collective-permute-start | bytes 1544 | tf_op jit(solution)/shard_map/ppermute | solution.py:356
  67.9 2.1 %collective-permute-done.9 = f32[32,4]{1,0:T(8,128)S(1)} collective-permute-done((f32[32,4]{1,0:T(8,128)S(1)}, f32[32,4]{1,0:T(8,128)S(1)}, u32[]{:S(2)}, u32[]{:S(2)}) %collective-permute-start.9) | collective-permute-done | bytes 544 | tf_op jit(solution)/shard_map/ppermute | solution.py:356
  69.9 0.7 copy.13
  (24 shorter events, 0.5 us)
Async XLA Ops:
  0.6 10.4 %copy-start.6 = (f32[4,12,8,8]{1,3,2,0:T(8,128)S(1)}, f32[4,12,8,8]{1,3,2,0:T(8,128)}, u32[]{:S(2)}) copy-start(f32[4,12,8,8]{1,3,2,0:T(8,128)} %param.5) | copy-start | bytes 36868
  0.6 11.4 %copy-start.1 = (f32[8,8]{1,0:T(8,128)S(1)}, f32[8,8]{1,0:T(8,128)}, u32[]{:S(2)}) copy-start(f32[8,8]{1,0:T(8,128)} %gamma_ref.1) | copy-start | bytes 772
  2.0 28.0 %collective-permute-start = (bf16[1,2,64,8,512]{4,3,2,1,0:T(8,128)(2,1)S(1)}, bf16[1,2,64,8,512]{4,3,2,1,0:T(8,128)(2,1)S(1)}, u32[]{:S(2)}, u32[]{:S(2)}) collective-permute-start(bf16[1,2,64,8,512]{4,3,2,1,0:T(8,128)(2,1)S(1)} %constant_dynamic-slice_fusion.6), channel_id=1, source_target_pairs={{0,24},{4,28},{8,16},{12,20},{16,8},{20,12},{24,0},{28,4},{1,25},{... | collective-permute-start | bytes 3145736 | tf_op jit(solution)/shard_map/ppermute | solution.py:292
  10.4 30.3 %collective-permute-start.1 = (bf16[1,1,64,8,512]{4,3,2,1,0:T(8,128)(2,1)}, bf16[1,1,64,8,512]{4,3,2,1,0:T(8,128)(2,1)S(1)}, u32[]{:S(2)}, u32[]{:S(2)}) collective-permute-start(bf16[1,1,64,8,512]{4,3,2,1,0:T(8,128)(2,1)} %get-tuple-element.20), channel_id=1, source_target_pairs={{0,8},{4,12},{8,0},{12,4},{16,24},{20,28},{24,16},{28,20},{1,9},{5... | collective-permute-start | bytes 1572872 | tf_op jit(solution)/shard_map/ppermute | solution.py:292
  11.0 29.7 %collective-permute-start.2 = (bf16[1,1,64,8,512]{4,3,2,1,0:T(8,128)(2,1)}, bf16[1,1,64,8,512]{4,3,2,1,0:T(8,128)(2,1)S(1)}, u32[]{:S(2)}, u32[]{:S(2)}) collective-permute-start(bf16[1,1,64,8,512]{4,3,2,1,0:T(8,128)(2,1)} %get-tuple-element.21), channel_id=1, source_target_pairs={{0,16},{4,20},{8,24},{12,28},{16,0},{20,4},{24,8},{28,12},{1,17},{... | collective-permute-start | bytes 1572872 | tf_op jit(solution)/shard_map/ppermute | solution.py:292
  15.1 2.2 %copy-start = (bf16[1,2,256,8,512]{4,3,2,1,0:T(8,128)(2,1)S(1)}, bf16[1,2,256,8,512]{4,3,2,1,0:T(8,128)(2,1)}, u32[]{:S(2)}) copy-start(bf16[1,2,256,8,512]{4,3,2,1,0:T(8,128)(2,1)} %refs_1_.1) | copy-start | bytes 12582916
  34.0 9.9 %copy-start.5 = (bf16[1,1,32,8,512]{4,3,2,1,0:T(8,128)(2,1)S(1)}, bf16[1,1,32,8,512]{4,3,2,1,0:T(8,128)(2,1)}, u32[]{:S(2)}) copy-start(bf16[1,1,32,8,512]{4,3,2,1,0:T(8,128)(2,1)} %get-tuple-element.24) | copy-start | bytes 786436
  34.0 11.5 %copy-start.4 = (bf16[1,1,32,8,512]{4,3,2,1,0:T(8,128)(2,1)S(1)}, bf16[1,1,32,8,512]{4,3,2,1,0:T(8,128)(2,1)}, u32[]{:S(2)}) copy-start(bf16[1,1,32,8,512]{4,3,2,1,0:T(8,128)(2,1)} %get-tuple-element.25) | copy-start | bytes 786436
  34.0 12.9 %copy-start.3 = (bf16[1,1,32,8,512]{4,3,2,1,0:T(8,128)(2,1)S(1)}, bf16[1,1,32,8,512]{4,3,2,1,0:T(8,128)(2,1)}, u32[]{:S(2)}) copy-start(bf16[1,1,32,8,512]{4,3,2,1,0:T(8,128)(2,1)} %get-tuple-element.26) | copy-start | bytes 786436
  34.1 12.9 %copy-start.2 = (bf16[1,1,32,8,512]{4,3,2,1,0:T(8,128)(2,1)S(1)}, bf16[1,1,32,8,512]{4,3,2,1,0:T(8,128)(2,1)}, u32[]{:S(2)}) copy-start(bf16[1,1,32,8,512]{4,3,2,1,0:T(8,128)(2,1)} %get-tuple-element.27) | copy-start | bytes 786436
  43.9 4.2 %collective-permute-start.3 = (f32[32,32,512]{2,1,0:T(8,128)S(1)}, f32[32,32,512]{2,1,0:T(8,128)S(1)}, u32[]{:S(2)}, u32[]{:S(2)}) collective-permute-start(f32[32,32,512]{2,1,0:T(8,128)S(1)} %get-tuple-element.23), channel_id=1, source_target_pairs={{0,4},{4,0},{8,12},{12,8},{16,20},{20,16},{24,28},{28,24},{1,5},{5... | collective-permute-start | bytes 6291464 | tf_op jit(solution)/shard_map/ppermute | solution.py:333
  43.9 9.2 %collective-permute-start.4 = (bf16[1,1,32,8,512]{4,3,2,1,0:T(8,128)(2,1)S(1)}, bf16[1,1,32,8,512]{4,3,2,1,0:T(8,128)(2,1)S(1)}, u32[]{:S(2)}, u32[]{:S(2)}) collective-permute-start(bf16[1,1,32,8,512]{4,3,2,1,0:T(8,128)(2,1)S(1)} %copy-done.5), channel_id=1, source_target_pairs={{0,8},{4,12},{8,0},{12,4},{16,24},{20,28},{24,16},{28,20},{1,9},{5... | collective-permute-start | bytes 786440 | tf_op jit(solution)/shard_map/ppermute | solution.py:292
  45.5 9.2 %collective-permute-start.5 = (bf16[1,1,32,8,512]{4,3,2,1,0:T(8,128)(2,1)S(1)}, bf16[1,1,32,8,512]{4,3,2,1,0:T(8,128)(2,1)S(1)}, u32[]{:S(2)}, u32[]{:S(2)}) collective-permute-start(bf16[1,1,32,8,512]{4,3,2,1,0:T(8,128)(2,1)S(1)} %copy-done.4), channel_id=1, source_target_pairs={{0,16},{4,20},{8,24},{12,28},{16,0},{20,4},{24,8},{28,12},{1,17},{... | collective-permute-start | bytes 786440 | tf_op jit(solution)/shard_map/ppermute | solution.py:292
  46.9 10.8 %collective-permute-start.6 = (bf16[1,1,32,8,512]{4,3,2,1,0:T(8,128)(2,1)S(1)}, bf16[1,1,32,8,512]{4,3,2,1,0:T(8,128)(2,1)S(1)}, u32[]{:S(2)}, u32[]{:S(2)}) collective-permute-start(bf16[1,1,32,8,512]{4,3,2,1,0:T(8,128)(2,1)S(1)} %copy-done.3), channel_id=1, source_target_pairs={{0,12},{4,8},{8,4},{12,0},{16,28},{20,24},{24,20},{28,16},{1,13},{... | collective-permute-start | bytes 786440 | tf_op jit(solution)/shard_map/ppermute | solution.py:292
  46.9 11.7 %collective-permute-start.7 = (bf16[1,1,32,8,512]{4,3,2,1,0:T(8,128)(2,1)S(1)}, bf16[1,1,32,8,512]{4,3,2,1,0:T(8,128)(2,1)S(1)}, u32[]{:S(2)}, u32[]{:S(2)}) collective-permute-start(bf16[1,1,32,8,512]{4,3,2,1,0:T(8,128)(2,1)S(1)} %copy-done.2), channel_id=1, source_target_pairs={{0,20},{4,16},{8,28},{12,24},{16,4},{20,0},{24,12},{28,8},{1,21},{... | collective-permute-start | bytes 786440 | tf_op jit(solution)/shard_map/ppermute | solution.py:292
  61.5 3.8 %collective-permute-start.8 = (f32[32,4]{1,0:T(8,128)S(1)}, f32[32,4]{1,0:T(8,128)S(1)}, u32[]{:S(2)}, u32[]{:S(2)}) collective-permute-start(f32[32,4]{1,0:T(8,128)S(1)} %get-tuple-element.29), channel_id=1, source_target_pairs={{0,1},{1,0},{2,3},{3,2},{4,5},{5,4},{6,7},{7,6},{8,9},{9,8},{10,11... | collective-permute-start | bytes 1544 | tf_op jit(solution)/shard_map/ppermute | solution.py:356
  65.3 4.6 %collective-permute-start.9 = (f32[32,4]{1,0:T(8,128)S(1)}, f32[32,4]{1,0:T(8,128)S(1)}, u32[]{:S(2)}, u32[]{:S(2)}) collective-permute-start(f32[32,4]{1,0:T(8,128)S(1)} %add.66), channel_id=1, source_target_pairs={{0,2},{1,3},{2,0},{3,1},{4,6},{5,7},{6,4},{7,5},{8,10},{9,11},{10,... | collective-permute-start | bytes 1544 | tf_op jit(solution)/shard_map/ppermute | solution.py:356

commit v2 on v1

--- a/solution.py
+++ b/solution.py
@@ -40,9 +40,11 @@
     return 0.5 * (right + right.T)
 
 
-def table_kernel(place_ref, gamma_ref, gamma_t_ref, encode_ref, lines_ref, extra_ref):
-    column = place_ref[0]
-    gamma, gamma_t = gamma_ref[...], gamma_t_ref[...]
+def table_kernel(nodes_here, gamma_ref, coeffs_ref, lines_ref, extra_ref):
+    column, _ = where_am_i(nodes_here)
+    gamma = gamma_ref[...]
+    gamma_t = gamma.T
+    encode = encode_rows(coeffs_ref[...])
     eye_rows = lax.broadcasted_iota(jnp.int32, (PLANES, PLANES), 0)
     eye_lanes = lax.broadcasted_iota(jnp.int32, (PLANES, PLANES), 1)
     identity = (eye_rows == eye_lanes).astype(jnp.float32)
@@ -78,7 +80,7 @@
         node = 4 * source + row
         return jnp.where((node < DATA_NODES - VIRTUAL) | (node >= DATA_NODES), 1.0, 0.0)
 
-    upto3 = jnp.concatenate([encode_ref[row] for row in range(3)], axis=0)
+    upto3 = jnp.concatenate(encode[:3], axis=0)
     for o in range(4):
         source = column ^ o
 
@@ -94,38 +96,55 @@
             for row in range(3):
                 piece = product[row * OUT_ROWS : (row + 1) * OUT_ROWS] * real(source, row)
                 lines_ref[row, o, j * OUT_ROWS : (j + 1) * OUT_ROWS] = parts(piece)
-            piece = dot32(encode_ref[3], jnp.where(from_own, own(column), zero))
+            piece = dot32(encode[3], jnp.where(from_own, own(column), zero))
             piece = piece * real(source, 3)
             lines_ref[3, o, j * OUT_ROWS : (j + 1) * OUT_ROWS] = parts(piece)
     away = jnp.where(block_in < column, from_upper, from_lower)
     away = jnp.where((block_in == (column ^ block_out)) & (block_out != 0), away, zero)
-    extra_ref[...] = parts(dot32(encode_ref[3], away) * real(column, 3))
-
-
-def build_tables(place, gamma, coeffs):
-    by_column = coeffs.reshape(PARITY, 3, 4, PLANES, PLANES)
-    data_part = -jnp.transpose(by_column, (2, 0, 3, 1, 4)).reshape(4, OUT_ROWS, 3 * PLANES)
-    own_parity = jnp.arange(OUT_ROWS)[None, :] - PLANES * jnp.arange(4)[:, None]
-    parity_part = (own_parity[:, :, None] == jnp.arange(PLANES)).astype(jnp.float32)
-    encode = jnp.concatenate([data_part, parity_part], axis=-1)
-    vmem = pl.BlockSpec(memory_space=pltpu.VMEM)
-    return pl.pallas_call(
-        table_kernel,
-        out_shape=(
+    extra_ref[...] = parts(dot32(encode[3], away) * real(column, 3))
+
+
+def encode_rows(coeffs):
+    nodes = coeffs.shape[-1]
+    flat = coeffs.reshape(OUT_ROWS * PLANES, nodes)
+    lanes = lax.broadcasted_iota(jnp.int32, (nodes, 4 * OUT_ROWS), 1)
+    node = 4 * ((lanes // PLANES) % 4) + lanes // OUT_ROWS
+    pick = lax.broadcasted_iota(jnp.int32, (nodes, 4 * OUT_ROWS), 0) == node
+    picked = dot32(flat, pick.astype(jnp.float32)).reshape(OUT_ROWS, PLANES, 4 * OUT_ROWS)
+    plane = lax.broadcasted_iota(jnp.int32, picked.shape, 1)
+    lane = lax.broadcasted_iota(jnp.int32, picked.shape, 2)
+    data = jnp.sum(jnp.where(plane == lane % PLANES, picked, 0.0), axis=1)
+    out = lax.broadcasted_iota(jnp.int32, (OUT_ROWS, 4 * PLANES), 0)
+    into = lax.broadcasted_iota(jnp.int32, (OUT_ROWS, 4 * PLANES), 1)
+    rows = []
+    for row in range(4):
+        parity = (into // PLANES == 3) & (out == row * PLANES + into % PLANES)
+        taken = data[:, row * OUT_ROWS : (row + 1) * OUT_ROWS]
+        rows.append(jnp.where(parity, 1.0, -taken))
+    return rows
+
+
+def build_tables(nodes_here, gamma, coeffs):
+    return kernel_call(
+        lambda *refs: table_kernel(nodes_here, *refs),
+        (
             jax.ShapeDtypeStruct((4, 4, 4 * OUT_ROWS, WIDTH), jnp.bfloat16),
             jax.ShapeDtypeStruct((OUT_ROWS, WIDTH), jnp.bfloat16),
         ),
-        in_specs=[pl.BlockSpec(memory_space=pltpu.SMEM), vmem, vmem, vmem],
-        out_specs=(vmem, vmem),
-        compiler_params=pltpu.CompilerParams(vmem_limit_bytes=16 * MIB),
-        name="tables",
-        cost_estimate=pl.CostEstimate(flops=1_000_000_000, bytes_accessed=MIB, transcendentals=0),
-    )(place, gamma, gamma.T, encode)
+        (gamma, jnp.transpose(coeffs, (0, 2, 3, 1))),
+        1000,
+        1,
+    )
+
+
+def where_am_i(nodes_here):
+    peers = 4 // nodes_here
+    device = lax.axis_index("node")
+    return device // peers, device % peers
 
 
 def gathered(slabs):
-    block = jnp.concatenate([slab.astype(jnp.float32) for slab in slabs], axis=0)
-    block = block.astype(jnp.bfloat16)
+    block = jnp.concatenate(slabs, axis=0)
     return jnp.concatenate([block] * PARTS, axis=0)
 
 
@@ -139,10 +158,10 @@
     return jnp.dot(matrix, gathered(slabs), preferred_element_type=jnp.float32)
 
 
-def own_kernel(layers_here, place_ref, own_ref, lines_ref, extra_ref, out_ref):
+def own_kernel(layers_here, own_ref, lines_ref, extra_ref, out_ref):
     nodes_here = own_ref.shape[1]
     column_layers = out_ref.shape[0]
-    column, peer = place_ref[0], place_ref[1]
+    column, peer = where_am_i(nodes_here)
     flip = peer * layers_here
     for local in range(nodes_here):
         row = peer * nodes_here + local
@@ -159,7 +178,7 @@
                 out_ref[spot] = value if local == 0 else out_ref[spot] + value
             return carry
 
-        lax.fori_loop(0, column_layers // 4, body, 0, unroll=2)
+        lax.fori_loop(0, column_layers // 4, body, 0, unroll=8)
 
     @pl.when((peer + 1) * nodes_here == 4)
     def _():
@@ -170,11 +189,11 @@
             out_ref[layer ^ flip] += mixed(extra_ref[...], away)
             return carry
 
-        lax.fori_loop(0, column_layers, body, 0, unroll=4)
-
-
-def add_rows(layers_here, nodes_here, place_ref, lines_ref, pieces, before_ref, total_ref):
-    peer = place_ref[1]
+        lax.fori_loop(0, column_layers, body, 0, unroll=8)
+
+
+def add_rows(layers_here, nodes_here, lines_ref, pieces, before_ref, total_ref):
+    _, peer = where_am_i(nodes_here)
     flip = peer * layers_here
     for order, (local, sources) in enumerate(pieces.items()):
         row = peer * nodes_here + local
@@ -191,39 +210,60 @@
                 total_ref[spot] = start + total[at * OUT_ROWS : (at + 1) * OUT_ROWS]
             return carry
 
-        lax.fori_loop(0, total_ref.shape[0] // 4, body, 0, unroll=2)
-
-
-def across_kernel(layers_here, nodes_here, place_ref, lines_ref, before_ref, far_ref, total_ref):
+        lax.fori_loop(0, total_ref.shape[0] // 4, body, 0, unroll=8)
+
+
+def across_kernel(layers_here, nodes_here, lines_ref, before_ref, far_ref, total_ref):
     pieces = {at: [(3, far_ref.at[:, pl.ds(at, 1)])] for at in range(nodes_here)}
-    add_rows(layers_here, nodes_here, place_ref, lines_ref, pieces, before_ref, total_ref)
-
-
-def beside_kernel(layers_here, nodes_here, rows, place_ref, lines_ref, before_ref, *refs):
+    add_rows(layers_here, nodes_here, lines_ref, pieces, before_ref, total_ref)
+
+
+def beside_kernel(layers_here, nodes_here, rows, lines_ref, before_ref, *refs):
     piece_refs, out_refs, total_ref = refs[: 2 * rows], refs[2 * rows : -1], refs[-1]
     pieces = {at: [(1, piece_refs[2 * at]), (2, piece_refs[2 * at + 1])] for at in range(rows)}
-    add_rows(layers_here, nodes_here, place_ref, lines_ref, pieces, before_ref, total_ref)
+    add_rows(layers_here, nodes_here, lines_ref, pieces, before_ref, total_ref)
     for slot in reversed(range(len(out_refs))):
 
         def copy(at, carry):
             out_refs[slot][at] = total_ref[slot * layers_here + at]
             return carry
 
-        lax.fori_loop(0, layers_here, copy, 0, unroll=4)
-
-
-def finish_kernel(nodes_here, place_ref, lines_ref, before_ref, *refs):
+        lax.fori_loop(0, layers_here, copy, 0, unroll=8)
+
+
+def join_kernel(nodes_here, sums_count, lines_ref, *refs):
+    sum_refs, piece_refs, total_ref = refs[:sums_count], refs[sums_count:-1], refs[-1]
+    _, peer = where_am_i(nodes_here)
+    row = peer * nodes_here + nodes_here - 1
+
+    def body(number, carry):
+        line = line_at(number, jnp.int32(1))
+        total = None
+        for order, ref in enumerate(piece_refs):
+            term = mixed(lines_ref[row, 1 + order % 2], [ref[0, 0, layer] for layer in line])
+            total = term if total is None else total + term
+        for at, layer in enumerate(line):
+            value = sum(ref[layer] for ref in sum_refs)
+            if total is not None:
+                value = value + total[at * OUT_ROWS : (at + 1) * OUT_ROWS]
+            total_ref[layer] = value
+        return carry
+
+    lax.fori_loop(0, total_ref.shape[0] // 4, body, 0, unroll=8)
+
+
+def finish_kernel(nodes_here, lines_ref, before_ref, *refs):
     piece_refs, refs = refs[:-5], refs[-5:]
     out_ref, energy_ref, value_ref, lanes_ref, sems = refs
     layers_here, _, byte_count = value_ref.shape
-    peer = place_ref[1]
+    _, peer = where_am_i(nodes_here)
     copies = []
     for first in range(0, layers_here, 16):
         for number in range(4):
             line = [first + number + 4 * at for at in range(4)]
             total = None
             for order, ref in enumerate(piece_refs):
-                row = (peer ^ (order // 2)) * nodes_here + nodes_here - 1
+                row = (peer ^ (1 + order // 2)) * nodes_here + nodes_here - 1
                 term = mixed(lines_ref[row, 1 + order % 2], [ref[0, 0, layer] for layer in line])
                 total = term if total is None else total + term
             for at, layer in enumerate(line):
@@ -241,24 +281,27 @@
         copy = pltpu.make_async_copy(value_ref.at[rows], out_ref.at[rows], sems.at[first // 16])
         copy.start()
         copies.append(copy)
-    sums = [jnp.sum(lanes_ref[i], axis=1, keepdims=True) for i in range(PARITY)]
-    energy_ref[...] = jnp.concatenate(sums, axis=1) * (1.0 / (PLANES * byte_count))
+    lanes = jnp.concatenate([lanes_ref[i] for i in range(PARITY)], axis=0)
+    energy = jnp.sum(lanes.T, axis=0, keepdims=True) * (1.0 / (PLANES * byte_count))
+    for i in range(PARITY):
+        energy_ref[0, i : i + 1] = energy[:, i * layers_here : (i + 1) * layers_here]
     for copy in copies:
         copy.wait()
 
 
-def kernel_call(body, out_shape, operands, mflops, mib, out_specs=None, scratch=()):
-    smem = pl.BlockSpec(memory_space=pltpu.SMEM)
-    vmem = pl.BlockSpec(memory_space=pltpu.VMEM)
+def kernel_call(
+    body, out_shape, operands, mflops, mib, in_specs=None, out_specs=None, scratch=(), vmem=16
+):
+    whole = pl.BlockSpec(memory_space=pltpu.VMEM)
     if out_specs is None:
-        out_specs = jax.tree.map(lambda _: vmem, out_shape)
+        out_specs = jax.tree.map(lambda _: whole, out_shape)
     return pl.pallas_call(
         body,
         out_shape=out_shape,
-        in_specs=[smem] + [vmem] * (len(operands) - 1),
+        in_specs=in_specs or [whole] * len(operands),
         out_specs=out_specs,
         scratch_shapes=scratch,
-        compiler_params=pltpu.CompilerParams(vmem_limit_bytes=24 * MIB),
+        compiler_params=pltpu.CompilerParams(vmem_limit_bytes=vmem * MIB),
         cost_estimate=pl.CostEstimate(
             flops=mflops * 1_000_000, bytes_accessed=mib * MIB, transcendentals=0
         ),
@@ -271,71 +314,95 @@
     peers = devices // 4
     layers_here = layers // devices
     column_layers = layers // 4
-    device = lax.axis_index("node")
-    column, peer = device // peers, device % peers
-    place = jnp.stack([column, peer]).astype(jnp.int32)
     direct = nodes_here == 2
     rows = nodes_here - 1 if direct else nodes_here
 
-    def cut(source, first_row, row_count, offset, slot=None):
-        first, count = (column ^ offset) * column_layers, column_layers
-        if slot is not None:
-            first, count = first + (peer ^ slot) * layers_here, layers_here
-        return lax.dynamic_slice(
-            source,
-            (0, first_row, first, 0, 0),
-            (stripes_here, row_count, count, planes, byte_count),
+    def cut(source, plan):
+        def body(source_ref, *refs):
+            column, peer = where_am_i(nodes_here)
+            out_refs, sems = refs[:-1], refs[-1]
+            copies = []
+            for at, (first_row, row_count, offset, slot) in enumerate(plan):
+                first, count = (column ^ offset) * column_layers, column_layers
+                if slot is not None:
+                    first, count = first + (peer ^ slot) * layers_here, layers_here
+                piece = source_ref.at[:, pl.ds(first_row, row_count), pl.ds(first, count)]
+                copies.append(pltpu.make_async_copy(piece, out_refs[at], sems.at[at]))
+                copies[-1].start()
+            for copy in copies:
+                copy.wait()
+
+        shapes = [
+            (stripes_here, count, column_layers if slot is None else layers_here, planes, byte_count)
+            for _, count, _, slot in plan
+        ]
+        return kernel_call(
+            body,
+            [jax.ShapeDtypeStruct(shape, groups.dtype) for shape in shapes],
+            (source,),
+            1,
+            3,
+            in_specs=[pl.BlockSpec(memory_space=pltpu.HBM)],
+            scratch=[pltpu.SemaphoreType.DMA((len(plan),))],
+            vmem=16,
         )
 
     def send(piece, offset, slot=0):
         route = [(i, (((i // peers) ^ offset) * peers + i % peers) ^ slot) for i in range(devices)]
         return lax.ppermute(piece, "node", route)
 
-    across_piece = cut(groups, 0, nodes_here, 3)
+    column = lax.axis_index("node") // peers
+    across_piece = lax.dynamic_slice(
+        groups,
+        (0, 0, (column ^ 3) * column_layers, 0, 0),
+        (stripes_here, nodes_here, column_layers, planes, byte_count),
+    )
     source, across_piece = lax.optimization_barrier((groups, across_piece))
     across_piece = send(across_piece, 3)
     plan = [(at, 1, offset, None) for at in range(rows) for offset in (1, 2)]
     if direct:
         plan += [(rows, 1, offset, slot) for slot in range(peers) for offset in (1, 2)]
-    cuts = [cut(source, *entry) for entry in plan]
-    cuts = lax.optimization_barrier(tuple(cuts))
+    cuts = cut(source, plan)
     arrived = [send(piece, entry[2], entry[3] or 0) for piece, entry in zip(cuts, plan)]
     beside_pieces, last_pieces = arrived[: 2 * rows], arrived[2 * rows :]
-    lines, extra = build_tables(place, gamma, coeffs)
+    lines, extra = build_tables(nodes_here, gamma, coeffs)
 
     all_layers = jax.ShapeDtypeStruct((column_layers, OUT_ROWS, byte_count), jnp.float32)
     part = jax.ShapeDtypeStruct((layers_here, OUT_ROWS, byte_count), jnp.float32)
     own = kernel_call(
-        lambda *refs: own_kernel(layers_here, *refs),
-        all_layers,
-        (place, groups, lines, extra),
-        2000,
-        8,
+        lambda *refs: own_kernel(layers_here, *refs), all_layers, (groups, lines, extra), 2000, 8
     )
     across = kernel_call(
         lambda *refs: across_kernel(layers_here, nodes_here, *refs),
         all_layers,
-        (place, lines, own, across_piece),
+        (lines, own, across_piece),
         2000,
         9,
     )
     sums = kernel_call(
         lambda *refs: beside_kernel(layers_here, nodes_here, rows, *refs),
         [part] * peers,
-        (place, lines, across, *beside_pieces),
+        (lines, across, *beside_pieces),
         2000,
         9,
         scratch=[pltpu.VMEM(all_layers.shape, jnp.float32)],
     )
-    total = sums[0]
+    parts = [sums[0]]
     for slot in range(1, peers):
         route = [(i, (i // peers) * peers + ((i % peers) ^ slot)) for i in range(devices)]
-        total = total + lax.ppermute(sums[slot], "node", route)
+        parts.append(lax.ppermute(sums[slot], "node", route))
+    total = kernel_call(
+        lambda *refs: join_kernel(nodes_here, peers, *refs),
+        part,
+        (lines, *parts, *last_pieces[:2]),
+        500,
+        6,
+    )
 
     syndrome, energy = kernel_call(
         lambda *refs: finish_kernel(nodes_here, *refs),
-        (part, jax.ShapeDtypeStruct((layers_here, PARITY), jnp.float32)),
-        (place, lines, total, *last_pieces),
+        (part, jax.ShapeDtypeStruct((stripes_here, PARITY, layers_here), jnp.float32)),
+        (lines, total, *last_pieces[2:]),
         500,
         4,
         out_specs=(
@@ -362,7 +429,7 @@
     scores = energy / (pool / (stripes * stripes_here) + epsilon)
     return (
         syndrome.reshape(layers_here, stripes_here, PARITY, planes, byte_count),
-        scores.reshape(layers_here, stripes_here, PARITY),
+        jnp.transpose(scores, (2, 0, 1)),
     )
 
 

time: 70.8 us -> 67.8 us (0.958)
  waiting for transfers between devices: 30 us -> 39.4 us
  Pallas kernels: 17 us -> 10.6 us
  local copies, waits for them, and re-layouts: 9.24 us -> 3.53 us
    ppermute x7, waiting for transfers between devices: 25.5 us -> 35.5 us  [send(): return lax.ppermute(piece, 'node', route)]
    pallas_call x5 -> x7, Pallas kernels: 17 us -> 10.6 us  [kernel_call(): pl.pallas_call(body, out_shape=out_shape, in_specs=in_specs or [whole] *...]
    dynamic_slice x3 -> x1, local copies, waits for them, and re-layouts: 5.77 us -> 1.34 us  [scrub(): lax.dynamic_slice(groups, (0, 0, (column ^ 3) * column_layers, 0, 0), (st...]
    unnamed x16 -> x8, local copies, waits for them, and re-layouts: 2.54 us -> 2.2 us
  transfers between devices with their start and end apart: 10 -> 10, of which waited for: 9 -> 8; matrix products, arithmetic and copies ran while one was open for 8% -> 0% of each run, Pallas kernels for 16% -> 11%
where the time goes in v2:
time: 67.8 us; the launch traced here: 67.7 us
  waiting for transfers between devices  39.4 us (58%)
  starting transfers between devices  12.8 us (19%)
  Pallas kernels  10.6 us (16%)
  local copies, waits for them, and re-layouts  3.53 us (5%)
  between operations  0.73 us (1%)
    ppermute x7, waiting for transfers between devices, send(): return lax.ppermute(piece, 'node', route)  35.5 us
    pallas_call x7, Pallas kernels, kernel_call(): pl.pallas_call(body, out_shape=out_shape, in_specs=in_specs or [whole] *...  10.6 us
    ppermute x7, starting transfers between devices, send(): return lax.ppermute(piece, 'node', route)  8.47 us
    ppermute x2, starting transfers between devices, scrub(): lax.ppermute(pool, 'stripe', [(i, i ^ distance) for i in range(stripes)])  4.25 us
    ppermute x2, waiting for transfers between devices, scrub(): lax.ppermute(pool, 'stripe', [(i, i ^ distance) for i in range(stripes)])  3.88 us
    unnamed x8, local copies, waits for them, and re-layouts  2.2 us
  transfers between devices with their start and end apart: 10, of which 8 were waited for; matrix products, arithmetic and copies ran while one was open for 0% of the time, Pallas kernels for 11%

profile of v2, /device:TPU:0, one launch (start us, length us, event | category | flops | bytes accessed | tf_op | source)
XLA Modules:
  0.0 67.7 jit_solution(14845441964716205953)
XLA Ops:
  0.6 0.0 copy-start.2
  0.7 1.3 %constant_dynamic-slice_fusion = bf16[1,2,64,8,512]{4,3,2,1,0:T(8,128)(2,1)S(1)} fusion(bf16[1,2,256,8,512]{4,3,2,1,0:T(8,128)(2,1)} %source_ref, s32[]{:T(128)S(6)} %select_n.9), kind=kLoop, calls=%fused_computation.2 | loop fusion | bytes 2097156 | tf_op jit(solution)/shard_map/dynamic_slice | solution.py:355
  2.0 4.0 %collective-permute-start = (bf16[1,2,64,8,512]{4,3,2,1,0:T(8,128)(2,1)S(1)}, bf16[1,2,64,8,512]{4,3,2,1,0:T(8,128)(2,1)S(1)}, u32[]{:S(2)}, u32[]{:S(2)}) collective-permute-start(bf16[1,2,64,8,512]{4,3,2,1,0:T(8,128)(2,1)S(1)} %constant_dynamic-slice_fusion), channel_id=1, source_target_pairs={{0,24},{4,28},{8,16},{12,20},{16,8},{20,12},{24,0},{28,4},{1,25},{... | collective-permute-start | bytes 3145736 | tf_op jit(solution)/shard_map/ppermute | solution.py:352
  6.0 2.2 %copy-done = bf16[1,2,256,8,512]{4,3,2,1,0:T(8,128)(2,1)S(1)} copy-done((bf16[1,2,256,8,512]{4,3,2,1,0:T(8,128)(2,1)S(1)}, bf16[1,2,256,8,512]{4,3,2,1,0:T(8,128)(2,1)}, u32[]{:S(2)}) %copy-start) | copy-done | bytes 4194328
  8.2 0.2 shard_map.53
  8.4 0.6 collective-permute-start.1
  9.0 0.0 collective-permute-start.2
  9.0 0.0 copy-done.2
  9.1 2.8 %shard_map.50 = (bf16[4,4,128,96]{3,2,1,0:T(8,128)(2,1)S(1)}, bf16[32,96]{1,0:T(8,128)(2,1)S(1)}) custom-call(f32[8,8]{1,0:T(8,128)S(1)} %copy-done.3, f32[4,8,8,12]{3,2,1,0:T(8,128)S(1)} %bitcast.6), custom_call_target="tpu_custom_call" | custom-call | flops 1000000000 | bytes 1048576 | tf_op jit(solution)/shard_map/pallas_call | solution.py:298
  11.9 1.7 %shard_map.51.refs_1_ = f32[64,32,512]{2,1,0:T(8,128)S(1)} custom-call(bf16[1,2,256,8,512]{4,3,2,1,0:T(8,128)(2,1)S(1)} %copy-done.1, bf16[4,4,128,96]{3,2,1,0:T(8,128)(2,1)S(1)} %get-tuple-element.16.refs_1_.refs_0_, bf16[32,96]{1,0:T(8,128)(2,1)S(1)} %get-tuple-element.17.refs_2_), custom_call_target="tpu_custom_call" | custom-call | flops 2000000000 | bytes 8388608 | tf_op jit(solution)/shard_map/pallas_call | solution.py:298
  13.6 16.4 %collective-permute-done.refs_2_ = bf16[1,2,64,8,512]{4,3,2,1,0:T(8,128)(2,1)S(1)} collective-permute-done((bf16[1,2,64,8,512]{4,3,2,1,0:T(8,128)(2,1)S(1)}, bf16[1,2,64,8,512]{4,3,2,1,0:T(8,128)(2,1)S(1)}, u32[]{:S(2)}, u32[]{:S(2)}) %collective-permute-start) | collective-permute-done | bytes 1048608 | tf_op jit(solution)/shard_map/ppermute | solution.py:352
  30.0 1.7 %shard_map.52.refs_1_ = f32[64,32,512]{2,1,0:T(8,128)S(1)} custom-call(bf16[4,4,128,96]{3,2,1,0:T(8,128)(2,1)S(1)} %get-tuple-element.16.refs_1_.refs_0_, f32[64,32,512]{2,1,0:T(8,128)S(1)} %shard_map.51.refs_1_, bf16[1,2,64,8,512]{4,3,2,1,0:T(8,128)(2,1)S(1)} %collective-permute-done.refs_2_), custom_call_target="tpu_custom_call" | custom-call | flops 2000000000 | bytes 9437184 | tf_op jit(solution)/shard_map/pallas_call | solution.py:298
  31.8 8.9 %collective-permute-done.1.refs_2_ = bf16[1,1,64,8,512]{4,3,2,1,0:T(8,128)(2,1)S(1)} collective-permute-done((bf16[1,1,64,8,512]{4,3,2,1,0:T(8,128)(2,1)S(1)}, bf16[1,1,64,8,512]{4,3,2,1,0:T(8,128)(2,1)S(1)}, u32[]{:S(2)}, u32[]{:S(2)}) %collective-permute-start.1) | collective-permute-done | bytes 524320 | tf_op jit(solution)/shard_map/ppermute | solution.py:352
  40.7 0.0 collective-permute-done.2.refs_3_
  40.7 1.7 %shard_map.54 = (f32[32,32,512]{2,1,0:T(8,128)S(1)}, f32[32,32,512]{2,1,0:T(8,128)S(1)}) custom-call(bf16[4,4,128,96]{3,2,1,0:T(8,128)(2,1)S(1)} %get-tuple-element.16.refs_1_.refs_0_, f32[64,32,512]{2,1,0:T(8,128)S(1)} %shard_map.52.refs_1_, bf16[1,1,64,8,512]{4,3,2,1,0:T(8,128)(2,1)S(1)} %collective-permute-done.1.refs_2_, ...), custom_call_target="tpu_custom_call" | custom-call | flops 2000000000 | bytes 9437184 | tf_op jit(solution)/shard_map/pallas_call | solution.py:298
  42.4 0.1 collective-permute-start.3
  42.5 1.6 %collective-permute-start.4 = (bf16[1,1,32,8,512]{4,3,2,1,0:T(8,128)(2,1)S(1)}, bf16[1,1,32,8,512]{4,3,2,1,0:T(8,128)(2,1)S(1)}, u32[]{:S(2)}, u32[]{:S(2)}) collective-permute-start(bf16[1,1,32,8,512]{4,3,2,1,0:T(8,128)(2,1)S(1)} %get-tuple-element.24), channel_id=1, source_target_pairs={{0,8},{4,12},{8,0},{12,4},{16,24},{20,28},{24,16},{28,20},{1,9},{5... | collective-permute-start | bytes 786440 | tf_op jit(solution)/shard_map/ppermute | solution.py:352
  44.0 1.4 %collective-permute-start.5 = (bf16[1,1,32,8,512]{4,3,2,1,0:T(8,128)(2,1)S(1)}, bf16[1,1,32,8,512]{4,3,2,1,0:T(8,128)(2,1)S(1)}, u32[]{:S(2)}, u32[]{:S(2)}) collective-permute-start(bf16[1,1,32,8,512]{4,3,2,1,0:T(8,128)(2,1)S(1)} %get-tuple-element.25), channel_id=1, source_target_pairs={{0,16},{4,20},{8,24},{12,28},{16,0},{20,4},{24,8},{28,12},{1,17},{... | collective-permute-start | bytes 786440 | tf_op jit(solution)/shard_map/ppermute | solution.py:352
  45.4 0.0 collective-permute-start.6
  45.4 0.9 %collective-permute-start.7 = (bf16[1,1,32,8,512]{4,3,2,1,0:T(8,128)(2,1)S(1)}, bf16[1,1,32,8,512]{4,3,2,1,0:T(8,128)(2,1)S(1)}, u32[]{:S(2)}, u32[]{:S(2)}) collective-permute-start(bf16[1,1,32,8,512]{4,3,2,1,0:T(8,128)(2,1)S(1)} %get-tuple-element.27), channel_id=1, source_target_pairs={{0,20},{4,16},{8,28},{12,24},{16,4},{20,0},{24,12},{28,8},{1,21},{... | collective-permute-start | bytes 786440 | tf_op jit(solution)/shard_map/ppermute | solution.py:352
  46.3 5.4 %collective-permute-done.4.refs_3_ = bf16[1,1,32,8,512]{4,3,2,1,0:T(8,128)(2,1)S(1)} collective-permute-done((bf16[1,1,32,8,512]{4,3,2,1,0:T(8,128)(2,1)S(1)}, bf16[1,1,32,8,512]{4,3,2,1,0:T(8,128)(2,1)S(1)}, u32[]{:S(2)}, u32[]{:S(2)}) %collective-permute-start.4) | collective-permute-done | bytes 262176 | tf_op jit(solution)/shard_map/ppermute | solution.py:352
  51.7 1.5 %collective-permute-done.5.refs_4_ = bf16[1,1,32,8,512]{4,3,2,1,0:T(8,128)(2,1)S(1)} collective-permute-done((bf16[1,1,32,8,512]{4,3,2,1,0:T(8,128)(2,1)S(1)}, bf16[1,1,32,8,512]{4,3,2,1,0:T(8,128)(2,1)S(1)}, u32[]{:S(2)}, u32[]{:S(2)}) %collective-permute-start.5) | collective-permute-done | bytes 262176 | tf_op jit(solution)/shard_map/ppermute | solution.py:352
  53.2 0.0 collective-permute-done.3.refs_2_
  53.2 0.7 %shard_map.55.refs_1_ = f32[32,32,512]{2,1,0:T(8,128)S(1)} custom-call(bf16[4,4,128,96]{3,2,1,0:T(8,128)(2,1)S(1)} %get-tuple-element.16.refs_1_.refs_0_, f32[32,32,512]{2,1,0:T(8,128)S(1)} %get-tuple-element.22.refs_1_, f32[32,32,512]{2,1,0:T(8,128)S(1)} %collective-permute-done.3.refs_2_, bf16[1,1,32,8,512]{4,3,2,1,0:T(8,128)(2,1)S(1)} %collective-permute-done.4.refs_3_, ...), custom_call_target="tpu_custom_call" | custom-call | flops 500000000 | bytes 6291456 | tf_op jit(solution)/shard_map/pallas_call | solution.py:298
  53.9 2.3 %collective-permute-done.6.refs_2_ = bf16[1,1,32,8,512]{4,3,2,1,0:T(8,128)(2,1)S(1)} collective-permute-done((bf16[1,1,32,8,512]{4,3,2,1,0:T(8,128)(2,1)S(1)}, bf16[1,1,32,8,512]{4,3,2,1,0:T(8,128)(2,1)S(1)}, u32[]{:S(2)}, u32[]{:S(2)}) %collective-permute-start.6) | collective-permute-done | bytes 262176 | tf_op jit(solution)/shard_map/ppermute | solution.py:352
  56.2 0.9 %collective-permute-done.7.refs_3_ = bf16[1,1,32,8,512]{4,3,2,1,0:T(8,128)(2,1)S(1)} collective-permute-done((bf16[1,1,32,8,512]{4,3,2,1,0:T(8,128)(2,1)S(1)}, bf16[1,1,32,8,512]{4,3,2,1,0:T(8,128)(2,1)S(1)}, u32[]{:S(2)}, u32[]{:S(2)}) %collective-permute-start.7) | collective-permute-done | bytes 262176 | tf_op jit(solution)/shard_map/ppermute | solution.py:352
  57.2 1.8 %shard_map.56 = (f32[32,32,512]{2,1,0:T(8,128)}, f32[1,4,32]{2,1,0:T(4,128)S(1)}) custom-call(bf16[4,4,128,96]{3,2,1,0:T(8,128)(2,1)S(1)} %get-tuple-element.16.refs_1_.refs_0_, f32[32,32,512]{2,1,0:T(8,128)S(1)} %shard_map.55.refs_1_, bf16[1,1,32,8,512]{4,3,2,1,0:T(8,128)(2,1)S(1)} %collective-permute-done.6.refs_2_, ...), custom_call_target="tpu_custom_call" | custom-call | flops 500000000 | bytes 4194304 | tf_op jit(solution)/shard_map/pallas_call | solution.py:298
  58.9 1.7 %collective-permute-start.8 = (f32[1,4,32]{2,1,0:T(4,128)S(1)}, f32[1,4,32]{2,1,0:T(4,128)S(1)}, u32[]{:S(2)}, u32[]{:S(2)}) collective-permute-start(f32[1,4,32]{2,1,0:T(4,128)S(1)} %get-tuple-element.29), channel_id=1, source_target_pairs={{0,1},{1,0},{2,3},{3,2},{4,5},{5,4},{6,7},{7,6},{8,9},{9,8},{10,11... | collective-permute-start | bytes 1544 | tf_op jit(solution)/shard_map/ppermute | solution.py:423
  60.6 2.0 %collective-permute-done.8 = f32[1,4,32]{2,1,0:T(4,128)S(1)} collective-permute-done((f32[1,4,32]{2,1,0:T(4,128)S(1)}, f32[1,4,32]{2,1,0:T(4,128)S(1)}, u32[]{:S(2)}, u32[]{:S(2)}) %collective-permute-start.8) | collective-permute-done | bytes 544 | tf_op jit(solution)/shard_map/ppermute | solution.py:423
  62.6 2.6 %collective-permute-start.9 = (f32[1,4,32]{2,1,0:T(4,128)S(1)}, f32[1,4,32]{2,1,0:T(4,128)S(1)}, u32[]{:S(2)}, u32[]{:S(2)}) collective-permute-start(f32[1,4,32]{2,1,0:T(4,128)S(1)} %add.17), channel_id=1, source_target_pairs={{0,2},{1,3},{2,0},{3,1},{4,6},{5,7},{6,4},{7,5},{8,10},{9,11},{10,... | collective-permute-start | bytes 1544 | tf_op jit(solution)/shard_map/ppermute | solution.py:423
  65.2 1.9 %collective-permute-done.9 = f32[1,4,32]{2,1,0:T(4,128)S(1)} collective-permute-done((f32[1,4,32]{2,1,0:T(4,128)S(1)}, f32[1,4,32]{2,1,0:T(4,128)S(1)}, u32[]{:S(2)}, u32[]{:S(2)}) %collective-permute-start.9) | collective-permute-done | bytes 544 | tf_op jit(solution)/shard_map/ppermute | solution.py:423
  67.1 0.6 fusion
  (6 shorter events, 0.0 us)
Async XLA Ops:
  0.6 8.4 %copy-start.2 = (f32[4,12,8,8]{1,3,2,0:T(8,128)S(1)}, f32[4,12,8,8]{1,3,2,0:T(8,128)}, u32[]{:S(2)}) copy-start(f32[4,12,8,8]{1,3,2,0:T(8,128)} %param.5) | copy-start | bytes 36868
  2.0 28.0 %collective-permute-start = (bf16[1,2,64,8,512]{4,3,2,1,0:T(8,128)(2,1)S(1)}, bf16[1,2,64,8,512]{4,3,2,1,0:T(8,128)(2,1)S(1)}, u32[]{:S(2)}, u32[]{:S(2)}) collective-permute-start(bf16[1,2,64,8,512]{4,3,2,1,0:T(8,128)(2,1)S(1)} %constant_dynamic-slice_fusion), channel_id=1, source_target_pairs={{0,24},{4,28},{8,16},{12,20},{16,8},{20,12},{24,0},{28,4},{1,25},{... | collective-permute-start | bytes 3145736 | tf_op jit(solution)/shard_map/ppermute | solution.py:352
  6.0 2.2 %copy-start = (bf16[1,2,256,8,512]{4,3,2,1,0:T(8,128)(2,1)S(1)}, bf16[1,2,256,8,512]{4,3,2,1,0:T(8,128)(2,1)}, u32[]{:S(2)}) copy-start(bf16[1,2,256,8,512]{4,3,2,1,0:T(8,128)(2,1)} %source_ref) | copy-start | bytes 12582916
  8.2 0.9 %copy-start.3 = (f32[8,8]{1,0:T(8,128)S(1)}, f32[8,8]{1,0:T(8,128)}, u32[]{:S(2)}) copy-start(f32[8,8]{1,0:T(8,128)} %refs_0_.2) | copy-start | bytes 772
  8.2 3.7 %copy-start.1 = (bf16[1,2,256,8,512]{4,3,2,1,0:T(8,128)(2,1)S(1)}, bf16[1,2,256,8,512]{4,3,2,1,0:T(8,128)(2,1)}, u32[]{:S(2)}) copy-start(bf16[1,2,256,8,512]{4,3,2,1,0:T(8,128)(2,1)} %source_ref) | copy-start | bytes 12582916
  8.4 32.3 %collective-permute-start.1 = (bf16[1,1,64,8,512]{4,3,2,1,0:T(8,128)(2,1)S(1)}, bf16[1,1,64,8,512]{4,3,2,1,0:T(8,128)(2,1)S(1)}, u32[]{:S(2)}, u32[]{:S(2)}) collective-permute-start(bf16[1,1,64,8,512]{4,3,2,1,0:T(8,128)(2,1)S(1)} %get-tuple-element.20), channel_id=1, source_target_pairs={{0,8},{4,12},{8,0},{12,4},{16,24},{20,28},{24,16},{28,20},{1,9},{5... | collective-permute-start | bytes 1572872 | tf_op jit(solution)/shard_map/ppermute | solution.py:352
  9.0 31.7 %collective-permute-start.2 = (bf16[1,1,64,8,512]{4,3,2,1,0:T(8,128)(2,1)S(1)}, bf16[1,1,64,8,512]{4,3,2,1,0:T(8,128)(2,1)S(1)}, u32[]{:S(2)}, u32[]{:S(2)}) collective-permute-start(bf16[1,1,64,8,512]{4,3,2,1,0:T(8,128)(2,1)S(1)} %get-tuple-element.21), channel_id=1, source_target_pairs={{0,16},{4,20},{8,24},{12,28},{16,0},{20,4},{24,8},{28,12},{1,17},{... | collective-permute-start | bytes 1572872 | tf_op jit(solution)/shard_map/ppermute | solution.py:352
  42.4 10.8 %collective-permute-start.3 = (f32[32,32,512]{2,1,0:T(8,128)S(1)}, f32[32,32,512]{2,1,0:T(8,128)S(1)}, u32[]{:S(2)}, u32[]{:S(2)}) collective-permute-start(f32[32,32,512]{2,1,0:T(8,128)S(1)} %get-tuple-element.23), channel_id=1, source_target_pairs={{0,4},{4,0},{8,12},{12,8},{16,20},{20,16},{24,28},{28,24},{1,5},{5... | collective-permute-start | bytes 6291464 | tf_op jit(solution)/shard_map/ppermute | solution.py:393
  42.5 9.2 %collective-permute-start.4 = (bf16[1,1,32,8,512]{4,3,2,1,0:T(8,128)(2,1)S(1)}, bf16[1,1,32,8,512]{4,3,2,1,0:T(8,128)(2,1)S(1)}, u32[]{:S(2)}, u32[]{:S(2)}) collective-permute-start(bf16[1,1,32,8,512]{4,3,2,1,0:T(8,128)(2,1)S(1)} %get-tuple-element.24), channel_id=1, source_target_pairs={{0,8},{4,12},{8,0},{12,4},{16,24},{20,28},{24,16},{28,20},{1,9},{5... | collective-permute-start | bytes 786440 | tf_op jit(solution)/shard_map/ppermute | solution.py:352
  44.0 9.2 %collective-permute-start.5 = (bf16[1,1,32,8,512]{4,3,2,1,0:T(8,128)(2,1)S(1)}, bf16[1,1,32,8,512]{4,3,2,1,0:T(8,128)(2,1)S(1)}, u32[]{:S(2)}, u32[]{:S(2)}) collective-permute-start(bf16[1,1,32,8,512]{4,3,2,1,0:T(8,128)(2,1)S(1)} %get-tuple-element.25), channel_id=1, source_target_pairs={{0,16},{4,20},{8,24},{12,28},{16,0},{20,4},{24,8},{28,12},{1,17},{... | collective-permute-start | bytes 786440 | tf_op jit(solution)/shard_map/ppermute | solution.py:352
  45.4 10.8 %collective-permute-start.6 = (bf16[1,1,32,8,512]{4,3,2,1,0:T(8,128)(2,1)S(1)}, bf16[1,1,32,8,512]{4,3,2,1,0:T(8,128)(2,1)S(1)}, u32[]{:S(2)}, u32[]{:S(2)}) collective-permute-start(bf16[1,1,32,8,512]{4,3,2,1,0:T(8,128)(2,1)S(1)} %get-tuple-element.26), channel_id=1, source_target_pairs={{0,12},{4,8},{8,4},{12,0},{16,28},{20,24},{24,20},{28,16},{1,13},{... | collective-permute-start | bytes 786440 | tf_op jit(solution)/shard_map/ppermute | solution.py:352
  45.4 11.7 %collective-permute-start.7 = (bf16[1,1,32,8,512]{4,3,2,1,0:T(8,128)(2,1)S(1)}, bf16[1,1,32,8,512]{4,3,2,1,0:T(8,128)(2,1)S(1)}, u32[]{:S(2)}, u32[]{:S(2)}) collective-permute-start(bf16[1,1,32,8,512]{4,3,2,1,0:T(8,128)(2,1)S(1)} %get-tuple-element.27), channel_id=1, source_target_pairs={{0,20},{4,16},{8,28},{12,24},{16,4},{20,0},{24,12},{28,8},{1,21},{... | collective-permute-start | bytes 786440 | tf_op jit(solution)/shard_map/ppermute | solution.py:352
  58.9 3.7 %collective-permute-start.8 = (f32[1,4,32]{2,1,0:T(4,128)S(1)}, f32[1,4,32]{2,1,0:T(4,128)S(1)}, u32[]{:S(2)}, u32[]{:S(2)}) collective-permute-start(f32[1,4,32]{2,1,0:T(4,128)S(1)} %get-tuple-element.29), channel_id=1, source_target_pairs={{0,1},{1,0},{2,3},{3,2},{4,5},{5,4},{6,7},{7,6},{8,9},{9,8},{10,11... | collective-permute-start | bytes 1544 | tf_op jit(solution)/shard_map/ppermute | solution.py:423
  62.6 4.5 %collective-permute-start.9 = (f32[1,4,32]{2,1,0:T(4,128)S(1)}, f32[1,4,32]{2,1,0:T(4,128)S(1)}, u32[]{:S(2)}, u32[]{:S(2)}) collective-permute-start(f32[1,4,32]{2,1,0:T(4,128)S(1)} %add.17), channel_id=1, source_target_pairs={{0,2},{1,3},{2,0},{3,1},{4,6},{5,7},{6,4},{7,5},{8,10},{9,11},{10,... | collective-permute-start | bytes 1544 | tf_op jit(solution)/shard_map/ppermute | solution.py:423

commit v3 on v2

--- a/solution.py
+++ b/solution.py
@@ -213,8 +213,9 @@
         lax.fori_loop(0, total_ref.shape[0] // 4, body, 0, unroll=8)
 
 
-def across_kernel(layers_here, nodes_here, lines_ref, before_ref, far_ref, total_ref):
-    pieces = {at: [(3, far_ref.at[:, pl.ds(at, 1)])] for at in range(nodes_here)}
+def across_kernel(layers_here, nodes_here, lines_ref, before_ref, *refs):
+    far_refs, total_ref = refs[:-1], refs[-1]
+    pieces = {at: [(3, ref)] for at, ref in enumerate(far_refs)}
     add_rows(layers_here, nodes_here, lines_ref, pieces, before_ref, total_ref)
 
 
@@ -252,22 +253,22 @@
     lax.fori_loop(0, total_ref.shape[0] // 4, body, 0, unroll=8)
 
 
-def finish_kernel(nodes_here, lines_ref, before_ref, *refs):
-    piece_refs, refs = refs[:-5], refs[-5:]
-    out_ref, energy_ref, value_ref, lanes_ref, sems = refs
-    layers_here, _, byte_count = value_ref.shape
+def finish_kernel(nodes_here, first, lines_ref, before_ref, *refs):
+    earlier = 1 if first else 0
+    piece_refs, refs = refs[: len(refs) - 3 - earlier], refs[len(refs) - 3 - earlier :]
+    value_ref, energy_ref, lanes_ref = refs[earlier:]
+    count, _, byte_count = value_ref.shape
     _, peer = where_am_i(nodes_here)
-    copies = []
-    for first in range(0, layers_here, 16):
+    for base in range(0, count, 16):
         for number in range(4):
-            line = [first + number + 4 * at for at in range(4)]
+            line = [base + number + 4 * at for at in range(4)]
             total = None
             for order, ref in enumerate(piece_refs):
                 row = (peer ^ (1 + order // 2)) * nodes_here + nodes_here - 1
                 term = mixed(lines_ref[row, 1 + order % 2], [ref[0, 0, layer] for layer in line])
                 total = term if total is None else total + term
             for at, layer in enumerate(line):
-                value = before_ref[layer]
+                value = before_ref[first + layer]
                 if total is not None:
                     value = value + total[at * OUT_ROWS : (at + 1) * OUT_ROWS]
                 value_ref[layer] = value
@@ -277,20 +278,24 @@
                     lanes_ref[i, layer : layer + 1] = jnp.sum(
                         lanes[i * PLANES : (i + 1) * PLANES], axis=0, keepdims=True
                     )
-        rows = pl.ds(first, 16)
-        copy = pltpu.make_async_copy(value_ref.at[rows], out_ref.at[rows], sems.at[first // 16])
-        copy.start()
-        copies.append(copy)
     lanes = jnp.concatenate([lanes_ref[i] for i in range(PARITY)], axis=0)
     energy = jnp.sum(lanes.T, axis=0, keepdims=True) * (1.0 / (PLANES * byte_count))
+    if first:
+        energy_ref[0, :, 0:first] = refs[0][0]
     for i in range(PARITY):
-        energy_ref[0, i : i + 1] = energy[:, i * layers_here : (i + 1) * layers_here]
-    for copy in copies:
-        copy.wait()
+        energy_ref[0, i : i + 1, first : first + count] = energy[:, i * count : (i + 1) * count]
+
+
+def store_kernel(first, value_ref, *refs):
+    out_ref, sem = refs[-2:]
+    rows = pl.ds(first, value_ref.shape[0])
+    copy = pltpu.make_async_copy(value_ref, out_ref.at[rows], sem)
+    copy.start()
+    copy.wait()
 
 
 def kernel_call(
-    body, out_shape, operands, mflops, mib, in_specs=None, out_specs=None, scratch=(), vmem=16
+    body, out_shape, operands, mflops, mib, in_specs=None, out_specs=None, scratch=(), vmem=16, aliases=None
 ):
     whole = pl.BlockSpec(memory_space=pltpu.VMEM)
     if out_specs is None:
@@ -301,6 +306,7 @@
         in_specs=in_specs or [whole] * len(operands),
         out_specs=out_specs,
         scratch_shapes=scratch,
+        input_output_aliases=aliases or {},
         compiler_params=pltpu.CompilerParams(vmem_limit_bytes=vmem * MIB),
         cost_estimate=pl.CostEstimate(
             flops=mflops * 1_000_000, bytes_accessed=mib * MIB, transcendentals=0
@@ -317,24 +323,26 @@
     direct = nodes_here == 2
     rows = nodes_here - 1 if direct else nodes_here
 
+    halves = 2 if direct else 1
+    half = layers_here // halves
+
     def cut(source, plan):
         def body(source_ref, *refs):
             column, peer = where_am_i(nodes_here)
             out_refs, sems = refs[:-1], refs[-1]
             copies = []
-            for at, (first_row, row_count, offset, slot) in enumerate(plan):
-                first, count = (column ^ offset) * column_layers, column_layers
+            for at, (row, offset, slot, start, count) in enumerate(plan):
+                first = (column ^ offset) * column_layers + start
                 if slot is not None:
-                    first, count = first + (peer ^ slot) * layers_here, layers_here
-                piece = source_ref.at[:, pl.ds(first_row, row_count), pl.ds(first, count)]
+                    first += (peer ^ slot) * layers_here
+                piece = source_ref.at[:, pl.ds(row, 1), pl.ds(first, count)]
                 copies.append(pltpu.make_async_copy(piece, out_refs[at], sems.at[at]))
                 copies[-1].start()
             for copy in copies:
                 copy.wait()
 
         shapes = [
-            (stripes_here, count, column_layers if slot is None else layers_here, planes, byte_count)
-            for _, count, _, slot in plan
+            (stripes_here, 1, count, planes, byte_count) for _, _, _, _, count in plan
         ]
         return kernel_call(
             body,
@@ -355,15 +363,22 @@
     across_piece = lax.dynamic_slice(
         groups,
         (0, 0, (column ^ 3) * column_layers, 0, 0),
-        (stripes_here, nodes_here, column_layers, planes, byte_count),
+        (stripes_here, 1, column_layers, planes, byte_count),
     )
     source, across_piece = lax.optimization_barrier((groups, across_piece))
     across_piece = send(across_piece, 3)
-    plan = [(at, 1, offset, None) for at in range(rows) for offset in (1, 2)]
+    plan = [(at, 3, None, 0, column_layers) for at in range(1, nodes_here)]
+    plan += [(at, offset, None, 0, column_layers) for at in range(rows) for offset in (1, 2)]
     if direct:
-        plan += [(rows, 1, offset, slot) for slot in range(peers) for offset in (1, 2)]
+        for slot in range(peers):
+            for start in range(0, layers_here, layers_here if slot == 0 else half):
+                count = layers_here if slot == 0 else half
+                plan += [(rows, offset, slot, start, count) for offset in (1, 2)]
     cuts = cut(source, plan)
-    arrived = [send(piece, entry[2], entry[3] or 0) for piece, entry in zip(cuts, plan)]
+    cuts = lax.optimization_barrier(tuple(cuts))
+    arrived = [send(piece, entry[1], entry[2] or 0) for piece, entry in zip(cuts, plan)]
+    across_pieces = [across_piece] + arrived[: nodes_here - 1]
+    arrived = arrived[nodes_here - 1 :]
     beside_pieces, last_pieces = arrived[: 2 * rows], arrived[2 * rows :]
     lines, extra = build_tables(nodes_here, gamma, coeffs)
 
@@ -375,7 +390,7 @@
     across = kernel_call(
         lambda *refs: across_kernel(layers_here, nodes_here, *refs),
         all_layers,
-        (lines, own, across_piece),
+        (lines, own, *across_pieces),
         2000,
         9,
     )
@@ -399,30 +414,42 @@
         6,
     )
 
-    syndrome, energy = kernel_call(
-        lambda *refs: finish_kernel(nodes_here, *refs),
-        (part, jax.ShapeDtypeStruct((stripes_here, PARITY, layers_here), jnp.float32)),
-        (lines, total, *last_pieces[2:]),
-        500,
-        4,
-        out_specs=(
-            pl.BlockSpec(memory_space=pl.ANY),
-            pl.BlockSpec(memory_space=pltpu.VMEM),
-        ),
-        scratch=[
-            pltpu.VMEM(part.shape, jnp.float32),
-            pltpu.VMEM((PARITY, layers_here, 128), jnp.float32),
-            pltpu.SemaphoreType.DMA((layers_here // 16,)),
-        ],
-    )
+    any_space = pl.BlockSpec(memory_space=pl.ANY)
+    whole = pl.BlockSpec(memory_space=pltpu.VMEM)
+    syndrome, energy = [], []
+    for at in range(halves):
+        value, new_energy = kernel_call(
+            lambda *refs: finish_kernel(nodes_here, at * half, *refs),
+            (
+                jax.ShapeDtypeStruct((half, OUT_ROWS, byte_count), jnp.float32),
+                jax.ShapeDtypeStruct((stripes_here, PARITY, (at + 1) * half), jnp.float32),
+            ),
+            (lines, total, *last_pieces[2 + 2 * at :: 2 * halves], *last_pieces[3 + 2 * at :: 2 * halves], *energy),
+            500,
+            4,
+            scratch=[pltpu.VMEM((PARITY, half, 128), jnp.float32)],
+        )
+        energy = [new_energy]
+        syndrome = [
+            kernel_call(
+                lambda *refs: store_kernel(at * half, *refs),
+                part,
+                (value, *syndrome),
+                1,
+                4,
+                in_specs=[whole] + [any_space] * at,
+                out_specs=any_space,
+                scratch=[pltpu.SemaphoreType.DMA(())],
+                aliases={1: 0} if at else None,
+            )
+        ]
+    (syndrome,), (energy,) = syndrome, energy
     stripes = lax.axis_size("stripe")
     pool = energy
     if stripes & (stripes - 1) == 0:
         distance = 1
         while distance < stripes:
-            pool = pool + lax.ppermute(
-                pool, "stripe", [(i, i ^ distance) for i in range(stripes)]
-            )
+            pool = pool + lax.ppermute(pool, "stripe", [(i, i ^ distance) for i in range(stripes)])
             distance *= 2
     else:
         pool = lax.psum(energy, "stripe")

time: 67.8 us -> 68 us (level)
  waiting for transfers between devices: 39.4 us -> 33.5 us
  starting transfers between devices: 12.8 us -> 16.9 us
  Pallas kernels: 10.6 us -> 12.8 us
    ppermute x7 -> x10, starting transfers between devices: 8.47 us -> 12.6 us  [send(): return lax.ppermute(piece, 'node', route)]
    ppermute x7 -> x10, waiting for transfers between devices: 35.5 us -> 31.5 us  [send(): return lax.ppermute(piece, 'node', route)]
    pallas_call x7 -> x10, Pallas kernels: 10.6 us -> 12.8 us  [kernel_call(): pl.pallas_call(body, out_shape=out_shape, in_specs=in_specs or [whole] *...]
    ppermute x2, waiting for transfers between devices: 3.88 us -> 2.01 us  [scrub(): lax.ppermute(pool, 'stripe', [(i, i ^ distance) for i in range(stripes)])]
  transfers between devices with their start and end apart: 10 -> 13, of which waited for: 8 -> 8; matrix products, arithmetic and copies ran while one was open for 0% -> 0% of each run, Pallas kernels for 11% -> 15%
where the time goes in v3:
time: 68 us; the launch traced here: 67.8 us
  waiting for transfers between devices  33.5 us (49%)
  starting transfers between devices  16.9 us (25%)
  Pallas kernels  12.8 us (19%)
  local copies, waits for them, and re-layouts  3.31 us (5%)
  between operations  0.77 us (1%)
    ppermute x10, waiting for transfers between devices, send(): return lax.ppermute(piece, 'node', route)  31.5 us
    pallas_call x10, Pallas kernels, kernel_call(): pl.pallas_call(body, out_shape=out_shape, in_specs=in_specs or [whole] *...  12.8 us
    ppermute x10, starting transfers between devices, send(): return lax.ppermute(piece, 'node', route)  12.6 us
    ppermute x2, starting transfers between devices, scrub(): lax.ppermute(pool, 'stripe', [(i, i ^ distance) for i in range(stripes)])  4.18 us
    unnamed x8, local copies, waits for them, and re-layouts  2.2 us
    ppermute x2, waiting for transfers between devices, scrub(): lax.ppermute(pool, 'stripe', [(i, i ^ distance) for i in range(stripes)])  2.01 us
  transfers between devices with their start and end apart: 13, of which 8 were waited for; matrix products, arithmetic and copies ran while one was open for 0% of the time, Pallas kernels for 15%

profile of v3, /device:TPU:0, one launch (start us, length us, event | category | flops | bytes accessed | tf_op | source)
XLA Modules:
  0.0 67.8 jit_solution(14245941675829320072)
XLA Ops:
  0.7 1.1 %constant_dynamic-slice_fusion = bf16[1,1,64,8,512]{4,3,2,1,0:T(8,128)(2,1)S(1)} fusion(bf16[1,2,256,8,512]{4,3,2,1,0:T(8,128)(2,1)} %source_ref, s32[]{:T(128)S(6)} %select_n.9), kind=kLoop, calls=%fused_computation.2 | loop fusion | bytes 1048580 | tf_op jit(solution)/shard_map/dynamic_slice | solution.py:363
  1.8 4.0 %collective-permute-start = (bf16[1,1,64,8,512]{4,3,2,1,0:T(8,128)(2,1)S(1)}, bf16[1,1,64,8,512]{4,3,2,1,0:T(8,128)(2,1)S(1)}, u32[]{:S(2)}, u32[]{:S(2)}) collective-permute-start(bf16[1,1,64,8,512]{4,3,2,1,0:T(8,128)(2,1)S(1)} %constant_dynamic-slice_fusion), channel_id=1, source_target_pairs={{0,24},{4,28},{8,16},{12,20},{16,8},{20,12},{24,0},{28,4},{1,25},{... | collective-permute-start | bytes 1572872 | tf_op jit(solution)/shard_map/ppermute | solution.py:360
  5.8 2.2 %copy-done = bf16[1,2,256,8,512]{4,3,2,1,0:T(8,128)(2,1)S(1)} copy-done((bf16[1,2,256,8,512]{4,3,2,1,0:T(8,128)(2,1)S(1)}, bf16[1,2,256,8,512]{4,3,2,1,0:T(8,128)(2,1)}, u32[]{:S(2)}) %copy-start) | copy-done | bytes 4194328
  8.0 0.9 %shard_map.52 = (bf16[1,1,64,8,512]{4,3,2,1,0:T(8,128)(2,1)S(1)}, bf16[1,1,64,8,512]{4,3,2,1,0:T(8,128)(2,1)S(1)}, bf16[1,1,64,8,512]{4,3,2,1,0:T(8,128)(2,1)S(1...) custom-call(bf16[1,2,256,8,512]{4,3,2,1,0:T(8,128)(2,1)S(1)} %copy-done), custom_call_target="tpu_custom_call" | custom-call | flops 1000000 | bytes 3145728 | tf_op jit(solution)/shard_map/pallas_call | solution.py:303
  8.9 0.1 collective-permute-start.1
  9.0 2.0 %collective-permute-start.2 = (bf16[1,1,64,8,512]{4,3,2,1,0:T(8,128)(2,1)S(1)}, bf16[1,1,64,8,512]{4,3,2,1,0:T(8,128)(2,1)S(1)}, u32[]{:S(2)}, u32[]{:S(2)}) collective-permute-start(bf16[1,1,64,8,512]{4,3,2,1,0:T(8,128)(2,1)S(1)} %get-tuple-element.26), channel_id=1, source_target_pairs={{0,8},{4,12},{8,0},{12,4},{16,24},{20,28},{24,16},{28,20},{1,9},{5... | collective-permute-start | bytes 1572872 | tf_op jit(solution)/shard_map/ppermute | solution.py:360
  10.9 1.5 %collective-permute-start.3 = (bf16[1,1,64,8,512]{4,3,2,1,0:T(8,128)(2,1)S(1)}, bf16[1,1,64,8,512]{4,3,2,1,0:T(8,128)(2,1)S(1)}, u32[]{:S(2)}, u32[]{:S(2)}) collective-permute-start(bf16[1,1,64,8,512]{4,3,2,1,0:T(8,128)(2,1)S(1)} %get-tuple-element.27), channel_id=1, source_target_pairs={{0,16},{4,20},{8,24},{12,28},{16,0},{20,4},{24,8},{28,12},{1,17},{... | collective-permute-start | bytes 1572872 | tf_op jit(solution)/shard_map/ppermute | solution.py:360
  12.4 2.8 %shard_map.50 = (bf16[4,4,128,96]{3,2,1,0:T(8,128)(2,1)S(1)}, bf16[32,96]{1,0:T(8,128)(2,1)S(1)}) custom-call(f32[8,8]{1,0:T(8,128)S(1)} %copy-done.3, f32[4,8,8,12]{3,2,1,0:T(8,128)S(1)} %bitcast.6), custom_call_target="tpu_custom_call" | custom-call | flops 1000000000 | bytes 1048576 | tf_op jit(solution)/shard_map/pallas_call | solution.py:303
  15.3 1.7 %shard_map.51.refs_1_ = f32[64,32,512]{2,1,0:T(8,128)S(1)} custom-call(bf16[1,2,256,8,512]{4,3,2,1,0:T(8,128)(2,1)S(1)} %copy-done.1, bf16[4,4,128,96]{3,2,1,0:T(8,128)(2,1)S(1)} %get-tuple-element.21.refs_1_.refs_0_, bf16[32,96]{1,0:T(8,128)(2,1)S(1)} %get-tuple-element.22.refs_2_), custom_call_target="tpu_custom_call" | custom-call | flops 2000000000 | bytes 8388608 | tf_op jit(solution)/shard_map/pallas_call | solution.py:303
  17.0 1.6 %collective-permute-done.refs_2_ = bf16[1,1,64,8,512]{4,3,2,1,0:T(8,128)(2,1)S(1)} collective-permute-done((bf16[1,1,64,8,512]{4,3,2,1,0:T(8,128)(2,1)S(1)}, bf16[1,1,64,8,512]{4,3,2,1,0:T(8,128)(2,1)S(1)}, u32[]{:S(2)}, u32[]{:S(2)}) %collective-permute-start) | collective-permute-done | bytes 524320 | tf_op jit(solution)/shard_map/ppermute | solution.py:360
  18.6 11.2 %collective-permute-done.1.refs_3_ = bf16[1,1,64,8,512]{4,3,2,1,0:T(8,128)(2,1)S(1)} collective-permute-done((bf16[1,1,64,8,512]{4,3,2,1,0:T(8,128)(2,1)S(1)}, bf16[1,1,64,8,512]{4,3,2,1,0:T(8,128)(2,1)S(1)}, u32[]{:S(2)}, u32[]{:S(2)}) %collective-permute-start.1) | collective-permute-done | bytes 524320 | tf_op jit(solution)/shard_map/ppermute | solution.py:360
  29.8 1.7 %shard_map.53.refs_1_ = f32[64,32,512]{2,1,0:T(8,128)S(1)} custom-call(bf16[4,4,128,96]{3,2,1,0:T(8,128)(2,1)S(1)} %get-tuple-element.21.refs_1_.refs_0_, f32[64,32,512]{2,1,0:T(8,128)S(1)} %shard_map.51.refs_1_, bf16[1,1,64,8,512]{4,3,2,1,0:T(8,128)(2,1)S(1)} %collective-permute-done.refs_2_, bf16[1,1,64,8,512]{4,3,2,1,0:T(8,128)(2,1)S(1)} %collective-permute-done.1.refs_3_), custom_call_target="tpu_custom_call" | custom-call | flops 2000000000 | bytes 9437184 | tf_op jit(solution)/shard_map/pallas_call | solution.py:303
  31.5 8.9 %collective-permute-done.2.refs_2_ = bf16[1,1,64,8,512]{4,3,2,1,0:T(8,128)(2,1)S(1)} collective-permute-done((bf16[1,1,64,8,512]{4,3,2,1,0:T(8,128)(2,1)S(1)}, bf16[1,1,64,8,512]{4,3,2,1,0:T(8,128)(2,1)S(1)}, u32[]{:S(2)}, u32[]{:S(2)}) %collective-permute-start.2) | collective-permute-done | bytes 524320 | tf_op jit(solution)/shard_map/ppermute | solution.py:360
  40.5 1.7 %shard_map.54 = (f32[32,32,512]{2,1,0:T(8,128)S(1)}, f32[32,32,512]{2,1,0:T(8,128)S(1)}) custom-call(bf16[4,4,128,96]{3,2,1,0:T(8,128)(2,1)S(1)} %get-tuple-element.21.refs_1_.refs_0_, f32[64,32,512]{2,1,0:T(8,128)S(1)} %shard_map.53.refs_1_, bf16[1,1,64,8,512]{4,3,2,1,0:T(8,128)(2,1)S(1)} %collective-permute-done.2.refs_2_, ...), custom_call_target="tpu_custom_call" | custom-call | flops 2000000000 | bytes 9437184 | tf_op jit(solution)/shard_map/pallas_call | solution.py:303
  42.2 1.6 %collective-permute-start.5 = (bf16[1,1,32,8,512]{4,3,2,1,0:T(8,128)(2,1)S(1)}, bf16[1,1,32,8,512]{4,3,2,1,0:T(8,128)(2,1)S(1)}, u32[]{:S(2)}, u32[]{:S(2)}) collective-permute-start(bf16[1,1,32,8,512]{4,3,2,1,0:T(8,128)(2,1)S(1)} %get-tuple-element.30), channel_id=1, source_target_pairs={{0,8},{4,12},{8,0},{12,4},{16,24},{20,28},{24,16},{28,20},{1,9},{5... | collective-permute-start | bytes 786440 | tf_op jit(solution)/shard_map/ppermute | solution.py:360
  43.8 1.4 %collective-permute-start.6 = (bf16[1,1,32,8,512]{4,3,2,1,0:T(8,128)(2,1)S(1)}, bf16[1,1,32,8,512]{4,3,2,1,0:T(8,128)(2,1)S(1)}, u32[]{:S(2)}, u32[]{:S(2)}) collective-permute-start(bf16[1,1,32,8,512]{4,3,2,1,0:T(8,128)(2,1)S(1)} %get-tuple-element.31), channel_id=1, source_target_pairs={{0,16},{4,20},{8,24},{12,28},{16,0},{20,4},{24,8},{28,12},{1,17},{... | collective-permute-start | bytes 786440 | tf_op jit(solution)/shard_map/ppermute | solution.py:360
  45.2 0.9 %collective-permute-start.10 = (bf16[1,1,16,8,512]{4,3,2,1,0:T(8,128)(2,1)S(1)}, bf16[1,1,16,8,512]{4,3,2,1,0:T(8,128)(2,1)S(1)}, u32[]{:S(2)}, u32[]{:S(2)}) collective-permute-start(bf16[1,1,16,8,512]{4,3,2,1,0:T(8,128)(2,1)S(1)} %get-tuple-element.35), channel_id=1, source_target_pairs={{0,20},{4,16},{8,28},{12,24},{16,4},{20,0},{24,12},{28,8},{1,21},{... | collective-permute-start | bytes 393224 | tf_op jit(solution)/shard_map/ppermute | solution.py:360
  46.1 5.4 %collective-permute-done.5.refs_3_ = bf16[1,1,32,8,512]{4,3,2,1,0:T(8,128)(2,1)S(1)} collective-permute-done((bf16[1,1,32,8,512]{4,3,2,1,0:T(8,128)(2,1)S(1)}, bf16[1,1,32,8,512]{4,3,2,1,0:T(8,128)(2,1)S(1)}, u32[]{:S(2)}, u32[]{:S(2)}) %collective-permute-start.5) | collective-permute-done | bytes 262176 | tf_op jit(solution)/shard_map/ppermute | solution.py:360
  51.5 0.1 collective-permute-start.7
  51.6 1.4 %collective-permute-done.6.refs_4_ = bf16[1,1,32,8,512]{4,3,2,1,0:T(8,128)(2,1)S(1)} collective-permute-done((bf16[1,1,32,8,512]{4,3,2,1,0:T(8,128)(2,1)S(1)}, bf16[1,1,32,8,512]{4,3,2,1,0:T(8,128)(2,1)S(1)}, u32[]{:S(2)}, u32[]{:S(2)}) %collective-permute-start.6) | collective-permute-done | bytes 262176 | tf_op jit(solution)/shard_map/ppermute | solution.py:360
  53.0 1.1 %collective-permute-start.8 = (bf16[1,1,16,8,512]{4,3,2,1,0:T(8,128)(2,1)S(1)}, bf16[1,1,16,8,512]{4,3,2,1,0:T(8,128)(2,1)S(1)}, u32[]{:S(2)}, u32[]{:S(2)}) collective-permute-start(bf16[1,1,16,8,512]{4,3,2,1,0:T(8,128)(2,1)S(1)} %get-tuple-element.33), channel_id=1, source_target_pairs={{0,20},{4,16},{8,28},{12,24},{16,4},{20,0},{24,12},{28,8},{1,21},{... | collective-permute-start | bytes 393224 | tf_op jit(solution)/shard_map/ppermute | solution.py:360
  54.1 0.7 %shard_map.55.refs_1_ = f32[32,32,512]{2,1,0:T(8,128)S(1)} custom-call(bf16[4,4,128,96]{3,2,1,0:T(8,128)(2,1)S(1)} %get-tuple-element.21.refs_1_.refs_0_, f32[32,32,512]{2,1,0:T(8,128)S(1)} %get-tuple-element.28.refs_1_, f32[32,32,512]{2,1,0:T(8,128)S(1)} %collective-permute-done.4.refs_2_, bf16[1,1,32,8,512]{4,3,2,1,0:T(8,128)(2,1)S(1)} %collective-permute-done.5.refs_3_, ...), custom_call_target="tpu_custom_call" | custom-call | flops 500000000 | bytes 6291456 | tf_op jit(solution)/shard_map/pallas_call | solution.py:303
  54.8 0.6 shard_map.56
  55.5 1.8 %collective-permute-done.7.refs_2_ = bf16[1,1,16,8,512]{4,3,2,1,0:T(8,128)(2,1)S(1)} collective-permute-done((bf16[1,1,16,8,512]{4,3,2,1,0:T(8,128)(2,1)S(1)}, bf16[1,1,16,8,512]{4,3,2,1,0:T(8,128)(2,1)S(1)}, u32[]{:S(2)}, u32[]{:S(2)}) %collective-permute-start.7) | collective-permute-done | bytes 131104 | tf_op jit(solution)/shard_map/ppermute | solution.py:360
  57.2 1.2 %collective-permute-done.8.refs_3_ = bf16[1,1,16,8,512]{4,3,2,1,0:T(8,128)(2,1)S(1)} collective-permute-done((bf16[1,1,16,8,512]{4,3,2,1,0:T(8,128)(2,1)S(1)}, bf16[1,1,16,8,512]{4,3,2,1,0:T(8,128)(2,1)S(1)}, u32[]{:S(2)}, u32[]{:S(2)}) %collective-permute-start.8) | collective-permute-done | bytes 131104 | tf_op jit(solution)/shard_map/ppermute | solution.py:360
  58.5 0.6 shard_map.57
  59.1 1.6 %collective-permute-start.11 = (f32[1,4,32]{2,1,0:T(4,128)S(1)}, f32[1,4,32]{2,1,0:T(4,128)S(1)}, u32[]{:S(2)}, u32[]{:S(2)}) collective-permute-start(f32[1,4,32]{2,1,0:T(4,128)S(1)} %get-tuple-element.39), channel_id=1, source_target_pairs={{0,1},{1,0},{2,3},{3,2},{4,5},{5,4},{6,7},{7,6},{8,9},{9,8},{10,11... | collective-permute-start | bytes 1544 | tf_op jit(solution)/shard_map/ppermute | solution.py:452
  60.7 2.0 %collective-permute-done.11 = f32[1,4,32]{2,1,0:T(4,128)S(1)} collective-permute-done((f32[1,4,32]{2,1,0:T(4,128)S(1)}, f32[1,4,32]{2,1,0:T(4,128)S(1)}, u32[]{:S(2)}, u32[]{:S(2)}) %collective-permute-start.11) | collective-permute-done | bytes 544 | tf_op jit(solution)/shard_map/ppermute | solution.py:452
  62.7 2.6 %collective-permute-start.12 = (f32[1,4,32]{2,1,0:T(4,128)S(1)}, f32[1,4,32]{2,1,0:T(4,128)S(1)}, u32[]{:S(2)}, u32[]{:S(2)}) collective-permute-start(f32[1,4,32]{2,1,0:T(4,128)S(1)} %add.17), channel_id=1, source_target_pairs={{0,2},{1,3},{2,0},{3,1},{4,6},{5,7},{6,4},{7,5},{8,10},{9,11},{10,... | collective-permute-start | bytes 1544 | tf_op jit(solution)/shard_map/ppermute | solution.py:452
  65.3 1.0 %shard_map.58.refs_1_ = f32[32,32,512]{2,1,0:T(8,128)} custom-call(f32[16,32,512]{2,1,0:T(8,128)S(1)} %get-tuple-element.38.refs_0_), custom_call_target="tpu_custom_call" | custom-call | flops 1000000 | bytes 4194304 | tf_op jit(solution)/shard_map/pallas_call | solution.py:303
  66.2 1.0 %shard_map.59 = f32[32,32,512]{2,1,0:T(8,128)} custom-call(f32[16,32,512]{2,1,0:T(8,128)S(1)} %get-tuple-element.37.refs_0_, f32[32,32,512]{2,1,0:T(8,128)} %shard_map.58.refs_1_), custom_call_target="tpu_custom_call", output_to_operand_aliasing={{}: (1, {})} | custom-call | flops 1000000 | bytes 4194304 | tf_op jit(solution)/shard_map/pallas_call | solution.py:303
  67.2 0.6 fusion
  (15 shorter events, 0.1 us)
Async XLA Ops:
  0.6 11.8 %copy-start.2 = (f32[4,12,8,8]{1,3,2,0:T(8,128)S(1)}, f32[4,12,8,8]{1,3,2,0:T(8,128)}, u32[]{:S(2)}) copy-start(f32[4,12,8,8]{1,3,2,0:T(8,128)} %param.5) | copy-start | bytes 36868
  1.8 16.9 %collective-permute-start = (bf16[1,1,64,8,512]{4,3,2,1,0:T(8,128)(2,1)S(1)}, bf16[1,1,64,8,512]{4,3,2,1,0:T(8,128)(2,1)S(1)}, u32[]{:S(2)}, u32[]{:S(2)}) collective-permute-start(bf16[1,1,64,8,512]{4,3,2,1,0:T(8,128)(2,1)S(1)} %constant_dynamic-slice_fusion), channel_id=1, source_target_pairs={{0,24},{4,28},{8,16},{12,20},{16,8},{20,12},{24,0},{28,4},{1,25},{... | collective-permute-start | bytes 1572872 | tf_op jit(solution)/shard_map/ppermute | solution.py:360
  5.8 2.2 %copy-start = (bf16[1,2,256,8,512]{4,3,2,1,0:T(8,128)(2,1)S(1)}, bf16[1,2,256,8,512]{4,3,2,1,0:T(8,128)(2,1)}, u32[]{:S(2)}) copy-start(bf16[1,2,256,8,512]{4,3,2,1,0:T(8,128)(2,1)} %source_ref) | copy-start | bytes 12582916
  8.0 4.5 %copy-start.3 = (f32[8,8]{1,0:T(8,128)S(1)}, f32[8,8]{1,0:T(8,128)}, u32[]{:S(2)}) copy-start(f32[8,8]{1,0:T(8,128)} %refs_0_.2) | copy-start | bytes 772
  8.0 7.3 %copy-start.1 = (bf16[1,2,256,8,512]{4,3,2,1,0:T(8,128)(2,1)S(1)}, bf16[1,2,256,8,512]{4,3,2,1,0:T(8,128)(2,1)}, u32[]{:S(2)}) copy-start(bf16[1,2,256,8,512]{4,3,2,1,0:T(8,128)(2,1)} %source_ref) | copy-start | bytes 12582916
  8.9 20.9 %collective-permute-start.1 = (bf16[1,1,64,8,512]{4,3,2,1,0:T(8,128)(2,1)S(1)}, bf16[1,1,64,8,512]{4,3,2,1,0:T(8,128)(2,1)S(1)}, u32[]{:S(2)}, u32[]{:S(2)}) collective-permute-start(bf16[1,1,64,8,512]{4,3,2,1,0:T(8,128)(2,1)S(1)} %get-tuple-element.25), channel_id=1, source_target_pairs={{0,24},{4,28},{8,16},{12,20},{16,8},{20,12},{24,0},{28,4},{1,25},{... | collective-permute-start | bytes 1572872 | tf_op jit(solution)/shard_map/ppermute | solution.py:360
  9.0 31.5 %collective-permute-start.2 = (bf16[1,1,64,8,512]{4,3,2,1,0:T(8,128)(2,1)S(1)}, bf16[1,1,64,8,512]{4,3,2,1,0:T(8,128)(2,1)S(1)}, u32[]{:S(2)}, u32[]{:S(2)}) collective-permute-start(bf16[1,1,64,8,512]{4,3,2,1,0:T(8,128)(2,1)S(1)} %get-tuple-element.26), channel_id=1, source_target_pairs={{0,8},{4,12},{8,0},{12,4},{16,24},{20,28},{24,16},{28,20},{1,9},{5... | collective-permute-start | bytes 1572872 | tf_op jit(solution)/shard_map/ppermute | solution.py:360
  10.9 29.5 %collective-permute-start.3 = (bf16[1,1,64,8,512]{4,3,2,1,0:T(8,128)(2,1)S(1)}, bf16[1,1,64,8,512]{4,3,2,1,0:T(8,128)(2,1)S(1)}, u32[]{:S(2)}, u32[]{:S(2)}) collective-permute-start(bf16[1,1,64,8,512]{4,3,2,1,0:T(8,128)(2,1)S(1)} %get-tuple-element.27), channel_id=1, source_target_pairs={{0,16},{4,20},{8,24},{12,28},{16,0},{20,4},{24,8},{28,12},{1,17},{... | collective-permute-start | bytes 1572872 | tf_op jit(solution)/shard_map/ppermute | solution.py:360
  42.2 12.0 %collective-permute-start.4 = (f32[32,32,512]{2,1,0:T(8,128)S(1)}, f32[32,32,512]{2,1,0:T(8,128)S(1)}, u32[]{:S(2)}, u32[]{:S(2)}) collective-permute-start(f32[32,32,512]{2,1,0:T(8,128)S(1)} %get-tuple-element.29), channel_id=1, source_target_pairs={{0,4},{4,0},{8,12},{12,8},{16,20},{20,16},{24,28},{28,24},{1,5},{5... | collective-permute-start | bytes 6291464 | tf_op jit(solution)/shard_map/ppermute | solution.py:408
  42.2 9.2 %collective-permute-start.5 = (bf16[1,1,32,8,512]{4,3,2,1,0:T(8,128)(2,1)S(1)}, bf16[1,1,32,8,512]{4,3,2,1,0:T(8,128)(2,1)S(1)}, u32[]{:S(2)}, u32[]{:S(2)}) collective-permute-start(bf16[1,1,32,8,512]{4,3,2,1,0:T(8,128)(2,1)S(1)} %get-tuple-element.30), channel_id=1, source_target_pairs={{0,8},{4,12},{8,0},{12,4},{16,24},{20,28},{24,16},{28,20},{1,9},{5... | collective-permute-start | bytes 786440 | tf_op jit(solution)/shard_map/ppermute | solution.py:360
  43.8 9.2 %collective-permute-start.6 = (bf16[1,1,32,8,512]{4,3,2,1,0:T(8,128)(2,1)S(1)}, bf16[1,1,32,8,512]{4,3,2,1,0:T(8,128)(2,1)S(1)}, u32[]{:S(2)}, u32[]{:S(2)}) collective-permute-start(bf16[1,1,32,8,512]{4,3,2,1,0:T(8,128)(2,1)S(1)} %get-tuple-element.31), channel_id=1, source_target_pairs={{0,16},{4,20},{8,24},{12,28},{16,0},{20,4},{24,8},{28,12},{1,17},{... | collective-permute-start | bytes 786440 | tf_op jit(solution)/shard_map/ppermute | solution.py:360
  45.2 9.6 %collective-permute-start.9 = (bf16[1,1,16,8,512]{4,3,2,1,0:T(8,128)(2,1)S(1)}, bf16[1,1,16,8,512]{4,3,2,1,0:T(8,128)(2,1)S(1)}, u32[]{:S(2)}, u32[]{:S(2)}) collective-permute-start(bf16[1,1,16,8,512]{4,3,2,1,0:T(8,128)(2,1)S(1)} %get-tuple-element.34), channel_id=1, source_target_pairs={{0,12},{4,8},{8,4},{12,0},{16,28},{20,24},{24,20},{28,16},{1,13},{... | collective-permute-start | bytes 393224 | tf_op jit(solution)/shard_map/ppermute | solution.py:360
  45.2 9.6 %collective-permute-start.10 = (bf16[1,1,16,8,512]{4,3,2,1,0:T(8,128)(2,1)S(1)}, bf16[1,1,16,8,512]{4,3,2,1,0:T(8,128)(2,1)S(1)}, u32[]{:S(2)}, u32[]{:S(2)}) collective-permute-start(bf16[1,1,16,8,512]{4,3,2,1,0:T(8,128)(2,1)S(1)} %get-tuple-element.35), channel_id=1, source_target_pairs={{0,20},{4,16},{8,28},{12,24},{16,4},{20,0},{24,12},{28,8},{1,21},{... | collective-permute-start | bytes 393224 | tf_op jit(solution)/shard_map/ppermute | solution.py:360
  51.5 5.8 %collective-permute-start.7 = (bf16[1,1,16,8,512]{4,3,2,1,0:T(8,128)(2,1)S(1)}, bf16[1,1,16,8,512]{4,3,2,1,0:T(8,128)(2,1)S(1)}, u32[]{:S(2)}, u32[]{:S(2)}) collective-permute-start(bf16[1,1,16,8,512]{4,3,2,1,0:T(8,128)(2,1)S(1)} %get-tuple-element.32), channel_id=1, source_target_pairs={{0,12},{4,8},{8,4},{12,0},{16,28},{20,24},{24,20},{28,16},{1,13},{... | collective-permute-start | bytes 393224 | tf_op jit(solution)/shard_map/ppermute | solution.py:360
  53.0 5.5 %collective-permute-start.8 = (bf16[1,1,16,8,512]{4,3,2,1,0:T(8,128)(2,1)S(1)}, bf16[1,1,16,8,512]{4,3,2,1,0:T(8,128)(2,1)S(1)}, u32[]{:S(2)}, u32[]{:S(2)}) collective-permute-start(bf16[1,1,16,8,512]{4,3,2,1,0:T(8,128)(2,1)S(1)} %get-tuple-element.33), channel_id=1, source_target_pairs={{0,20},{4,16},{8,28},{12,24},{16,4},{20,0},{24,12},{28,8},{1,21},{... | collective-permute-start | bytes 393224 | tf_op jit(solution)/shard_map/ppermute | solution.py:360
  59.1 3.6 %collective-permute-start.11 = (f32[1,4,32]{2,1,0:T(4,128)S(1)}, f32[1,4,32]{2,1,0:T(4,128)S(1)}, u32[]{:S(2)}, u32[]{:S(2)}) collective-permute-start(f32[1,4,32]{2,1,0:T(4,128)S(1)} %get-tuple-element.39), channel_id=1, source_target_pairs={{0,1},{1,0},{2,3},{3,2},{4,5},{5,4},{6,7},{7,6},{8,9},{9,8},{10,11... | collective-permute-start | bytes 1544 | tf_op jit(solution)/shard_map/ppermute | solution.py:452
  62.7 4.6 %collective-permute-start.12 = (f32[1,4,32]{2,1,0:T(4,128)S(1)}, f32[1,4,32]{2,1,0:T(4,128)S(1)}, u32[]{:S(2)}, u32[]{:S(2)}) collective-permute-start(f32[1,4,32]{2,1,0:T(4,128)S(1)} %add.17), channel_id=1, source_target_pairs={{0,2},{1,3},{2,0},{3,1},{4,6},{5,7},{6,4},{7,5},{8,10},{9,11},{10,... | collective-permute-start | bytes 1544 | tf_op jit(solution)/shard_map/ppermute | solution.py:452

commit v4 on v3

--- a/solution.py
+++ b/solution.py
@@ -221,7 +221,7 @@
 
 def beside_kernel(layers_here, nodes_here, rows, lines_ref, before_ref, *refs):
     piece_refs, out_refs, total_ref = refs[: 2 * rows], refs[2 * rows : -1], refs[-1]
-    pieces = {at: [(1, piece_refs[2 * at]), (2, piece_refs[2 * at + 1])] for at in range(rows)}
+    pieces = {at: [(2, piece_refs[2 * at]), (1, piece_refs[2 * at + 1])] for at in range(rows)}
     add_rows(layers_here, nodes_here, lines_ref, pieces, before_ref, total_ref)
     for slot in reversed(range(len(out_refs))):
 
@@ -241,7 +241,7 @@
         line = line_at(number, jnp.int32(1))
         total = None
         for order, ref in enumerate(piece_refs):
-            term = mixed(lines_ref[row, 1 + order % 2], [ref[0, 0, layer] for layer in line])
+            term = mixed(lines_ref[row, 2 - order % 2], [ref[0, 0, layer] for layer in line])
             total = term if total is None else total + term
         for at, layer in enumerate(line):
             value = sum(ref[layer] for ref in sum_refs)
@@ -265,7 +265,7 @@
             total = None
             for order, ref in enumerate(piece_refs):
                 row = (peer ^ (1 + order // 2)) * nodes_here + nodes_here - 1
-                term = mixed(lines_ref[row, 1 + order % 2], [ref[0, 0, layer] for layer in line])
+                term = mixed(lines_ref[row, 2 - order % 2], [ref[0, 0, layer] for layer in line])
                 total = term if total is None else total + term
             for at, layer in enumerate(line):
                 value = before_ref[first + layer]
@@ -368,12 +368,12 @@
     source, across_piece = lax.optimization_barrier((groups, across_piece))
     across_piece = send(across_piece, 3)
     plan = [(at, 3, None, 0, column_layers) for at in range(1, nodes_here)]
-    plan += [(at, offset, None, 0, column_layers) for at in range(rows) for offset in (1, 2)]
+    plan += [(at, offset, None, 0, column_layers) for at in range(rows) for offset in (2, 1)]
     if direct:
         for slot in range(peers):
             for start in range(0, layers_here, layers_here if slot == 0 else half):
                 count = layers_here if slot == 0 else half
-                plan += [(rows, offset, slot, start, count) for offset in (1, 2)]
+                plan += [(rows, offset, slot, start, count) for offset in (2, 1)]
     cuts = cut(source, plan)
     cuts = lax.optimization_barrier(tuple(cuts))
     arrived = [send(piece, entry[1], entry[2] or 0) for piece, entry in zip(cuts, plan)]

time: 68 us -> 67.9 us (level)
  transfers between devices with their start and end apart: 13 -> 13, of which waited for: 8 -> 9; matrix products, arithmetic and copies ran while one was open for 0% -> 0% of each run, Pallas kernels for 15% -> 15%
where the time goes in v4:
time: 67.9 us; the launch traced here: 67.8 us
  waiting for transfers between devices  33.4 us (49%)
  starting transfers between devices  16.9 us (25%)
  Pallas kernels  12.8 us (19%)
  local copies, waits for them, and re-layouts  3.31 us (5%)
  between operations  0.77 us (1%)
    ppermute x10, waiting for transfers between devices, send(): return lax.ppermute(piece, 'node', route)  31.4 us
    pallas_call x10, Pallas kernels, kernel_call(): pl.pallas_call(body, out_shape=out_shape, in_specs=in_specs or [whole] *...  12.8 us
    ppermute x10, starting transfers between devices, send(): return lax.ppermute(piece, 'node', route)  12.7 us
    ppermute x2, starting transfers between devices, scrub(): lax.ppermute(pool, 'stripe', [(i, i ^ distance) for i in range(stripes)])  4.18 us
    unnamed x8, local copies, waits for them, and re-layouts  2.2 us
    ppermute x2, waiting for transfers between devices, scrub(): lax.ppermute(pool, 'stripe', [(i, i ^ distance) for i in range(stripes)])  2.01 us
  transfers between devices with their start and end apart: 13, of which 9 were waited for; matrix products, arithmetic and copies ran while one was open for 0% of the time, Pallas kernels for 15%

profile of v4, /device:TPU:0, one launch (start us, length us, event | category | flops | bytes accessed | tf_op | source)
XLA Modules:
  0.0 67.8 jit_solution(5533669037024951037)
XLA Ops:
  0.7 1.1 %constant_dynamic-slice_fusion = bf16[1,1,64,8,512]{4,3,2,1,0:T(8,128)(2,1)S(1)} fusion(bf16[1,2,256,8,512]{4,3,2,1,0:T(8,128)(2,1)} %source_ref, s32[]{:T(128)S(6)} %select_n.9), kind=kLoop, calls=%fused_computation.2 | loop fusion | bytes 1048580 | tf_op jit(solution)/shard_map/dynamic_slice | solution.py:363
  1.8 4.0 %collective-permute-start = (bf16[1,1,64,8,512]{4,3,2,1,0:T(8,128)(2,1)S(1)}, bf16[1,1,64,8,512]{4,3,2,1,0:T(8,128)(2,1)S(1)}, u32[]{:S(2)}, u32[]{:S(2)}) collective-permute-start(bf16[1,1,64,8,512]{4,3,2,1,0:T(8,128)(2,1)S(1)} %constant_dynamic-slice_fusion), channel_id=1, source_target_pairs={{0,24},{4,28},{8,16},{12,20},{16,8},{20,12},{24,0},{28,4},{1,25},{... | collective-permute-start | bytes 1572872 | tf_op jit(solution)/shard_map/ppermute | solution.py:360
  5.8 2.2 %copy-done = bf16[1,2,256,8,512]{4,3,2,1,0:T(8,128)(2,1)S(1)} copy-done((bf16[1,2,256,8,512]{4,3,2,1,0:T(8,128)(2,1)S(1)}, bf16[1,2,256,8,512]{4,3,2,1,0:T(8,128)(2,1)}, u32[]{:S(2)}) %copy-start) | copy-done | bytes 4194328
  8.0 0.9 %shard_map.52 = (bf16[1,1,64,8,512]{4,3,2,1,0:T(8,128)(2,1)S(1)}, bf16[1,1,64,8,512]{4,3,2,1,0:T(8,128)(2,1)S(1)}, bf16[1,1,64,8,512]{4,3,2,1,0:T(8,128)(2,1)S(1...) custom-call(bf16[1,2,256,8,512]{4,3,2,1,0:T(8,128)(2,1)S(1)} %copy-done), custom_call_target="tpu_custom_call" | custom-call | flops 1000000 | bytes 3145728 | tf_op jit(solution)/shard_map/pallas_call | solution.py:303
  8.9 0.1 collective-permute-start.1
  9.0 2.0 %collective-permute-start.2 = (bf16[1,1,64,8,512]{4,3,2,1,0:T(8,128)(2,1)S(1)}, bf16[1,1,64,8,512]{4,3,2,1,0:T(8,128)(2,1)S(1)}, u32[]{:S(2)}, u32[]{:S(2)}) collective-permute-start(bf16[1,1,64,8,512]{4,3,2,1,0:T(8,128)(2,1)S(1)} %get-tuple-element.26), channel_id=1, source_target_pairs={{0,16},{4,20},{8,24},{12,28},{16,0},{20,4},{24,8},{28,12},{1,17},{... | collective-permute-start | bytes 1572872 | tf_op jit(solution)/shard_map/ppermute | solution.py:360
  10.9 1.5 %collective-permute-start.3 = (bf16[1,1,64,8,512]{4,3,2,1,0:T(8,128)(2,1)S(1)}, bf16[1,1,64,8,512]{4,3,2,1,0:T(8,128)(2,1)S(1)}, u32[]{:S(2)}, u32[]{:S(2)}) collective-permute-start(bf16[1,1,64,8,512]{4,3,2,1,0:T(8,128)(2,1)S(1)} %get-tuple-element.27), channel_id=1, source_target_pairs={{0,8},{4,12},{8,0},{12,4},{16,24},{20,28},{24,16},{28,20},{1,9},{5... | collective-permute-start | bytes 1572872 | tf_op jit(solution)/shard_map/ppermute | solution.py:360
  12.4 2.8 %shard_map.50 = (bf16[4,4,128,96]{3,2,1,0:T(8,128)(2,1)S(1)}, bf16[32,96]{1,0:T(8,128)(2,1)S(1)}) custom-call(f32[8,8]{1,0:T(8,128)S(1)} %copy-done.3, f32[4,8,8,12]{3,2,1,0:T(8,128)S(1)} %bitcast.6), custom_call_target="tpu_custom_call" | custom-call | flops 1000000000 | bytes 1048576 | tf_op jit(solution)/shard_map/pallas_call | solution.py:303
  15.3 1.7 %shard_map.51.refs_1_ = f32[64,32,512]{2,1,0:T(8,128)S(1)} custom-call(bf16[1,2,256,8,512]{4,3,2,1,0:T(8,128)(2,1)S(1)} %copy-done.1, bf16[4,4,128,96]{3,2,1,0:T(8,128)(2,1)S(1)} %get-tuple-element.21.refs_1_.refs_0_, bf16[32,96]{1,0:T(8,128)(2,1)S(1)} %get-tuple-element.22.refs_2_), custom_call_target="tpu_custom_call" | custom-call | flops 2000000000 | bytes 8388608 | tf_op jit(solution)/shard_map/pallas_call | solution.py:303
  17.0 1.6 %collective-permute-done.refs_2_ = bf16[1,1,64,8,512]{4,3,2,1,0:T(8,128)(2,1)S(1)} collective-permute-done((bf16[1,1,64,8,512]{4,3,2,1,0:T(8,128)(2,1)S(1)}, bf16[1,1,64,8,512]{4,3,2,1,0:T(8,128)(2,1)S(1)}, u32[]{:S(2)}, u32[]{:S(2)}) %collective-permute-start) | collective-permute-done | bytes 524320 | tf_op jit(solution)/shard_map/ppermute | solution.py:360
  18.6 11.2 %collective-permute-done.1.refs_3_ = bf16[1,1,64,8,512]{4,3,2,1,0:T(8,128)(2,1)S(1)} collective-permute-done((bf16[1,1,64,8,512]{4,3,2,1,0:T(8,128)(2,1)S(1)}, bf16[1,1,64,8,512]{4,3,2,1,0:T(8,128)(2,1)S(1)}, u32[]{:S(2)}, u32[]{:S(2)}) %collective-permute-start.1) | collective-permute-done | bytes 524320 | tf_op jit(solution)/shard_map/ppermute | solution.py:360
  29.8 1.7 %shard_map.53.refs_1_ = f32[64,32,512]{2,1,0:T(8,128)S(1)} custom-call(bf16[4,4,128,96]{3,2,1,0:T(8,128)(2,1)S(1)} %get-tuple-element.21.refs_1_.refs_0_, f32[64,32,512]{2,1,0:T(8,128)S(1)} %shard_map.51.refs_1_, bf16[1,1,64,8,512]{4,3,2,1,0:T(8,128)(2,1)S(1)} %collective-permute-done.refs_2_, bf16[1,1,64,8,512]{4,3,2,1,0:T(8,128)(2,1)S(1)} %collective-permute-done.1.refs_3_), custom_call_target="tpu_custom_call" | custom-call | flops 2000000000 | bytes 9437184 | tf_op jit(solution)/shard_map/pallas_call | solution.py:303
  31.5 8.6 %collective-permute-done.2.refs_2_ = bf16[1,1,64,8,512]{4,3,2,1,0:T(8,128)(2,1)S(1)} collective-permute-done((bf16[1,1,64,8,512]{4,3,2,1,0:T(8,128)(2,1)S(1)}, bf16[1,1,64,8,512]{4,3,2,1,0:T(8,128)(2,1)S(1)}, u32[]{:S(2)}, u32[]{:S(2)}) %collective-permute-start.2) | collective-permute-done | bytes 524320 | tf_op jit(solution)/shard_map/ppermute | solution.py:360
  40.2 0.3 collective-permute-done.3.refs_3_
  40.5 1.7 %shard_map.54 = (f32[32,32,512]{2,1,0:T(8,128)S(1)}, f32[32,32,512]{2,1,0:T(8,128)S(1)}) custom-call(bf16[4,4,128,96]{3,2,1,0:T(8,128)(2,1)S(1)} %get-tuple-element.21.refs_1_.refs_0_, f32[64,32,512]{2,1,0:T(8,128)S(1)} %shard_map.53.refs_1_, bf16[1,1,64,8,512]{4,3,2,1,0:T(8,128)(2,1)S(1)} %collective-permute-done.2.refs_2_, ...), custom_call_target="tpu_custom_call" | custom-call | flops 2000000000 | bytes 9437184 | tf_op jit(solution)/shard_map/pallas_call | solution.py:303
  42.2 1.5 %collective-permute-start.5 = (bf16[1,1,32,8,512]{4,3,2,1,0:T(8,128)(2,1)S(1)}, bf16[1,1,32,8,512]{4,3,2,1,0:T(8,128)(2,1)S(1)}, u32[]{:S(2)}, u32[]{:S(2)}) collective-permute-start(bf16[1,1,32,8,512]{4,3,2,1,0:T(8,128)(2,1)S(1)} %get-tuple-element.30), channel_id=1, source_target_pairs={{0,16},{4,20},{8,24},{12,28},{16,0},{20,4},{24,8},{28,12},{1,17},{... | collective-permute-start | bytes 786440 | tf_op jit(solution)/shard_map/ppermute | solution.py:360
  43.7 1.5 %collective-permute-start.6 = (bf16[1,1,32,8,512]{4,3,2,1,0:T(8,128)(2,1)S(1)}, bf16[1,1,32,8,512]{4,3,2,1,0:T(8,128)(2,1)S(1)}, u32[]{:S(2)}, u32[]{:S(2)}) collective-permute-start(bf16[1,1,32,8,512]{4,3,2,1,0:T(8,128)(2,1)S(1)} %get-tuple-element.31), channel_id=1, source_target_pairs={{0,8},{4,12},{8,0},{12,4},{16,24},{20,28},{24,16},{28,20},{1,9},{5... | collective-permute-start | bytes 786440 | tf_op jit(solution)/shard_map/ppermute | solution.py:360
  45.3 0.8 %collective-permute-start.10 = (bf16[1,1,16,8,512]{4,3,2,1,0:T(8,128)(2,1)S(1)}, bf16[1,1,16,8,512]{4,3,2,1,0:T(8,128)(2,1)S(1)}, u32[]{:S(2)}, u32[]{:S(2)}) collective-permute-start(bf16[1,1,16,8,512]{4,3,2,1,0:T(8,128)(2,1)S(1)} %get-tuple-element.35), channel_id=1, source_target_pairs={{0,12},{4,8},{8,4},{12,0},{16,28},{20,24},{24,20},{28,16},{1,13},{... | collective-permute-start | bytes 393224 | tf_op jit(solution)/shard_map/ppermute | solution.py:360
  46.1 5.4 %collective-permute-done.5.refs_3_ = bf16[1,1,32,8,512]{4,3,2,1,0:T(8,128)(2,1)S(1)} collective-permute-done((bf16[1,1,32,8,512]{4,3,2,1,0:T(8,128)(2,1)S(1)}, bf16[1,1,32,8,512]{4,3,2,1,0:T(8,128)(2,1)S(1)}, u32[]{:S(2)}, u32[]{:S(2)}) %collective-permute-start.5) | collective-permute-done | bytes 262176 | tf_op jit(solution)/shard_map/ppermute | solution.py:360
  51.5 1.4 %collective-permute-done.6.refs_4_ = bf16[1,1,32,8,512]{4,3,2,1,0:T(8,128)(2,1)S(1)} collective-permute-done((bf16[1,1,32,8,512]{4,3,2,1,0:T(8,128)(2,1)S(1)}, bf16[1,1,32,8,512]{4,3,2,1,0:T(8,128)(2,1)S(1)}, u32[]{:S(2)}, u32[]{:S(2)}) %collective-permute-start.6) | collective-permute-done | bytes 262176 | tf_op jit(solution)/shard_map/ppermute | solution.py:360
  52.9 1.2 %collective-permute-start.8 = (bf16[1,1,16,8,512]{4,3,2,1,0:T(8,128)(2,1)S(1)}, bf16[1,1,16,8,512]{4,3,2,1,0:T(8,128)(2,1)S(1)}, u32[]{:S(2)}, u32[]{:S(2)}) collective-permute-start(bf16[1,1,16,8,512]{4,3,2,1,0:T(8,128)(2,1)S(1)} %get-tuple-element.33), channel_id=1, source_target_pairs={{0,12},{4,8},{8,4},{12,0},{16,28},{20,24},{24,20},{28,16},{1,13},{... | collective-permute-start | bytes 393224 | tf_op jit(solution)/shard_map/ppermute | solution.py:360
  54.1 0.7 %shard_map.55.refs_1_ = f32[32,32,512]{2,1,0:T(8,128)S(1)} custom-call(bf16[4,4,128,96]{3,2,1,0:T(8,128)(2,1)S(1)} %get-tuple-element.21.refs_1_.refs_0_, f32[32,32,512]{2,1,0:T(8,128)S(1)} %get-tuple-element.28.refs_1_, f32[32,32,512]{2,1,0:T(8,128)S(1)} %collective-permute-done.4.refs_2_, bf16[1,1,32,8,512]{4,3,2,1,0:T(8,128)(2,1)S(1)} %collective-permute-done.5.refs_3_, ...), custom_call_target="tpu_custom_call" | custom-call | flops 500000000 | bytes 6291456 | tf_op jit(solution)/shard_map/pallas_call | solution.py:303
  54.9 0.6 shard_map.56
  55.5 1.8 %collective-permute-done.7.refs_2_ = bf16[1,1,16,8,512]{4,3,2,1,0:T(8,128)(2,1)S(1)} collective-permute-done((bf16[1,1,16,8,512]{4,3,2,1,0:T(8,128)(2,1)S(1)}, bf16[1,1,16,8,512]{4,3,2,1,0:T(8,128)(2,1)S(1)}, u32[]{:S(2)}, u32[]{:S(2)}) %collective-permute-start.7) | collective-permute-done | bytes 131104 | tf_op jit(solution)/shard_map/ppermute | solution.py:360
  57.2 1.1 %collective-permute-done.8.refs_3_ = bf16[1,1,16,8,512]{4,3,2,1,0:T(8,128)(2,1)S(1)} collective-permute-done((bf16[1,1,16,8,512]{4,3,2,1,0:T(8,128)(2,1)S(1)}, bf16[1,1,16,8,512]{4,3,2,1,0:T(8,128)(2,1)S(1)}, u32[]{:S(2)}, u32[]{:S(2)}) %collective-permute-start.8) | collective-permute-done | bytes 131104 | tf_op jit(solution)/shard_map/ppermute | solution.py:360
  58.4 0.6 shard_map.57
  59.0 1.6 %collective-permute-start.11 = (f32[1,4,32]{2,1,0:T(4,128)S(1)}, f32[1,4,32]{2,1,0:T(4,128)S(1)}, u32[]{:S(2)}, u32[]{:S(2)}) collective-permute-start(f32[1,4,32]{2,1,0:T(4,128)S(1)} %get-tuple-element.39), channel_id=1, source_target_pairs={{0,1},{1,0},{2,3},{3,2},{4,5},{5,4},{6,7},{7,6},{8,9},{9,8},{10,11... | collective-permute-start | bytes 1544 | tf_op jit(solution)/shard_map/ppermute | solution.py:452
  60.6 2.0 %collective-permute-done.11 = f32[1,4,32]{2,1,0:T(4,128)S(1)} collective-permute-done((f32[1,4,32]{2,1,0:T(4,128)S(1)}, f32[1,4,32]{2,1,0:T(4,128)S(1)}, u32[]{:S(2)}, u32[]{:S(2)}) %collective-permute-start.11) | collective-permute-done | bytes 544 | tf_op jit(solution)/shard_map/ppermute | solution.py:452
  62.6 2.6 %collective-permute-start.12 = (f32[1,4,32]{2,1,0:T(4,128)S(1)}, f32[1,4,32]{2,1,0:T(4,128)S(1)}, u32[]{:S(2)}, u32[]{:S(2)}) collective-permute-start(f32[1,4,32]{2,1,0:T(4,128)S(1)} %add.17), channel_id=1, source_target_pairs={{0,2},{1,3},{2,0},{3,1},{4,6},{5,7},{6,4},{7,5},{8,10},{9,11},{10,... | collective-permute-start | bytes 1544 | tf_op jit(solution)/shard_map/ppermute | solution.py:452
  65.2 1.0 %shard_map.58.refs_1_ = f32[32,32,512]{2,1,0:T(8,128)} custom-call(f32[16,32,512]{2,1,0:T(8,128)S(1)} %get-tuple-element.38.refs_0_), custom_call_target="tpu_custom_call" | custom-call | flops 1000000 | bytes 4194304 | tf_op jit(solution)/shard_map/pallas_call | solution.py:303
  66.2 1.0 %shard_map.59 = f32[32,32,512]{2,1,0:T(8,128)} custom-call(f32[16,32,512]{2,1,0:T(8,128)S(1)} %get-tuple-element.37.refs_0_, f32[32,32,512]{2,1,0:T(8,128)} %shard_map.58.refs_1_), custom_call_target="tpu_custom_call", output_to_operand_aliasing={{}: (1, {})} | custom-call | flops 1000000 | bytes 4194304 | tf_op jit(solution)/shard_map/pallas_call | solution.py:303
  67.2 0.6 fusion
  (15 shorter events, 0.2 us)
Async XLA Ops:
  0.6 11.8 %copy-start.2 = (f32[4,12,8,8]{1,3,2,0:T(8,128)S(1)}, f32[4,12,8,8]{1,3,2,0:T(8,128)}, u32[]{:S(2)}) copy-start(f32[4,12,8,8]{1,3,2,0:T(8,128)} %param.5) | copy-start | bytes 36868
  1.8 16.9 %collective-permute-start = (bf16[1,1,64,8,512]{4,3,2,1,0:T(8,128)(2,1)S(1)}, bf16[1,1,64,8,512]{4,3,2,1,0:T(8,128)(2,1)S(1)}, u32[]{:S(2)}, u32[]{:S(2)}) collective-permute-start(bf16[1,1,64,8,512]{4,3,2,1,0:T(8,128)(2,1)S(1)} %constant_dynamic-slice_fusion), channel_id=1, source_target_pairs={{0,24},{4,28},{8,16},{12,20},{16,8},{20,12},{24,0},{28,4},{1,25},{... | collective-permute-start | bytes 1572872 | tf_op jit(solution)/shard_map/ppermute | solution.py:360
  5.8 2.2 %copy-start = (bf16[1,2,256,8,512]{4,3,2,1,0:T(8,128)(2,1)S(1)}, bf16[1,2,256,8,512]{4,3,2,1,0:T(8,128)(2,1)}, u32[]{:S(2)}) copy-start(bf16[1,2,256,8,512]{4,3,2,1,0:T(8,128)(2,1)} %source_ref) | copy-start | bytes 12582916
  8.0 4.5 %copy-start.3 = (f32[8,8]{1,0:T(8,128)S(1)}, f32[8,8]{1,0:T(8,128)}, u32[]{:S(2)}) copy-start(f32[8,8]{1,0:T(8,128)} %refs_0_.2) | copy-start | bytes 772
  8.0 7.3 %copy-start.1 = (bf16[1,2,256,8,512]{4,3,2,1,0:T(8,128)(2,1)S(1)}, bf16[1,2,256,8,512]{4,3,2,1,0:T(8,128)(2,1)}, u32[]{:S(2)}) copy-start(bf16[1,2,256,8,512]{4,3,2,1,0:T(8,128)(2,1)} %source_ref) | copy-start | bytes 12582916
  8.9 20.9 %collective-permute-start.1 = (bf16[1,1,64,8,512]{4,3,2,1,0:T(8,128)(2,1)S(1)}, bf16[1,1,64,8,512]{4,3,2,1,0:T(8,128)(2,1)S(1)}, u32[]{:S(2)}, u32[]{:S(2)}) collective-permute-start(bf16[1,1,64,8,512]{4,3,2,1,0:T(8,128)(2,1)S(1)} %get-tuple-element.25), channel_id=1, source_target_pairs={{0,24},{4,28},{8,16},{12,20},{16,8},{20,12},{24,0},{28,4},{1,25},{... | collective-permute-start | bytes 1572872 | tf_op jit(solution)/shard_map/ppermute | solution.py:360
  9.0 31.2 %collective-permute-start.2 = (bf16[1,1,64,8,512]{4,3,2,1,0:T(8,128)(2,1)S(1)}, bf16[1,1,64,8,512]{4,3,2,1,0:T(8,128)(2,1)S(1)}, u32[]{:S(2)}, u32[]{:S(2)}) collective-permute-start(bf16[1,1,64,8,512]{4,3,2,1,0:T(8,128)(2,1)S(1)} %get-tuple-element.26), channel_id=1, source_target_pairs={{0,16},{4,20},{8,24},{12,28},{16,0},{20,4},{24,8},{28,12},{1,17},{... | collective-permute-start | bytes 1572872 | tf_op jit(solution)/shard_map/ppermute | solution.py:360
  10.9 29.5 %collective-permute-start.3 = (bf16[1,1,64,8,512]{4,3,2,1,0:T(8,128)(2,1)S(1)}, bf16[1,1,64,8,512]{4,3,2,1,0:T(8,128)(2,1)S(1)}, u32[]{:S(2)}, u32[]{:S(2)}) collective-permute-start(bf16[1,1,64,8,512]{4,3,2,1,0:T(8,128)(2,1)S(1)} %get-tuple-element.27), channel_id=1, source_target_pairs={{0,8},{4,12},{8,0},{12,4},{16,24},{20,28},{24,16},{28,20},{1,9},{5... | collective-permute-start | bytes 1572872 | tf_op jit(solution)/shard_map/ppermute | solution.py:360
  42.1 12.0 %collective-permute-start.4 = (f32[32,32,512]{2,1,0:T(8,128)S(1)}, f32[32,32,512]{2,1,0:T(8,128)S(1)}, u32[]{:S(2)}, u32[]{:S(2)}) collective-permute-start(f32[32,32,512]{2,1,0:T(8,128)S(1)} %get-tuple-element.29), channel_id=1, source_target_pairs={{0,4},{4,0},{8,12},{12,8},{16,20},{20,16},{24,28},{28,24},{1,5},{5... | collective-permute-start | bytes 6291464 | tf_op jit(solution)/shard_map/ppermute | solution.py:408
  42.2 9.2 %collective-permute-start.5 = (bf16[1,1,32,8,512]{4,3,2,1,0:T(8,128)(2,1)S(1)}, bf16[1,1,32,8,512]{4,3,2,1,0:T(8,128)(2,1)S(1)}, u32[]{:S(2)}, u32[]{:S(2)}) collective-permute-start(bf16[1,1,32,8,512]{4,3,2,1,0:T(8,128)(2,1)S(1)} %get-tuple-element.30), channel_id=1, source_target_pairs={{0,16},{4,20},{8,24},{12,28},{16,0},{20,4},{24,8},{28,12},{1,17},{... | collective-permute-start | bytes 786440 | tf_op jit(solution)/shard_map/ppermute | solution.py:360
  43.7 9.2 %collective-permute-start.6 = (bf16[1,1,32,8,512]{4,3,2,1,0:T(8,128)(2,1)S(1)}, bf16[1,1,32,8,512]{4,3,2,1,0:T(8,128)(2,1)S(1)}, u32[]{:S(2)}, u32[]{:S(2)}) collective-permute-start(bf16[1,1,32,8,512]{4,3,2,1,0:T(8,128)(2,1)S(1)} %get-tuple-element.31), channel_id=1, source_target_pairs={{0,8},{4,12},{8,0},{12,4},{16,24},{20,28},{24,16},{28,20},{1,9},{5... | collective-permute-start | bytes 786440 | tf_op jit(solution)/shard_map/ppermute | solution.py:360
  45.2 9.6 %collective-permute-start.9 = (bf16[1,1,16,8,512]{4,3,2,1,0:T(8,128)(2,1)S(1)}, bf16[1,1,16,8,512]{4,3,2,1,0:T(8,128)(2,1)S(1)}, u32[]{:S(2)}, u32[]{:S(2)}) collective-permute-start(bf16[1,1,16,8,512]{4,3,2,1,0:T(8,128)(2,1)S(1)} %get-tuple-element.34), channel_id=1, source_target_pairs={{0,20},{4,16},{8,28},{12,24},{16,4},{20,0},{24,12},{28,8},{1,21},{... | collective-permute-start | bytes 393224 | tf_op jit(solution)/shard_map/ppermute | solution.py:360
  45.3 9.6 %collective-permute-start.10 = (bf16[1,1,16,8,512]{4,3,2,1,0:T(8,128)(2,1)S(1)}, bf16[1,1,16,8,512]{4,3,2,1,0:T(8,128)(2,1)S(1)}, u32[]{:S(2)}, u32[]{:S(2)}) collective-permute-start(bf16[1,1,16,8,512]{4,3,2,1,0:T(8,128)(2,1)S(1)} %get-tuple-element.35), channel_id=1, source_target_pairs={{0,12},{4,8},{8,4},{12,0},{16,28},{20,24},{24,20},{28,16},{1,13},{... | collective-permute-start | bytes 393224 | tf_op jit(solution)/shard_map/ppermute | solution.py:360
  51.5 5.8 %collective-permute-start.7 = (bf16[1,1,16,8,512]{4,3,2,1,0:T(8,128)(2,1)S(1)}, bf16[1,1,16,8,512]{4,3,2,1,0:T(8,128)(2,1)S(1)}, u32[]{:S(2)}, u32[]{:S(2)}) collective-permute-start(bf16[1,1,16,8,512]{4,3,2,1,0:T(8,128)(2,1)S(1)} %get-tuple-element.32), channel_id=1, source_target_pairs={{0,20},{4,16},{8,28},{12,24},{16,4},{20,0},{24,12},{28,8},{1,21},{... | collective-permute-start | bytes 393224 | tf_op jit(solution)/shard_map/ppermute | solution.py:360
  52.9 5.5 %collective-permute-start.8 = (bf16[1,1,16,8,512]{4,3,2,1,0:T(8,128)(2,1)S(1)}, bf16[1,1,16,8,512]{4,3,2,1,0:T(8,128)(2,1)S(1)}, u32[]{:S(2)}, u32[]{:S(2)}) collective-permute-start(bf16[1,1,16,8,512]{4,3,2,1,0:T(8,128)(2,1)S(1)} %get-tuple-element.33), channel_id=1, source_target_pairs={{0,12},{4,8},{8,4},{12,0},{16,28},{20,24},{24,20},{28,16},{1,13},{... | collective-permute-start | bytes 393224 | tf_op jit(solution)/shard_map/ppermute | solution.py:360
  59.0 3.6 %collective-permute-start.11 = (f32[1,4,32]{2,1,0:T(4,128)S(1)}, f32[1,4,32]{2,1,0:T(4,128)S(1)}, u32[]{:S(2)}, u32[]{:S(2)}) collective-permute-start(f32[1,4,32]{2,1,0:T(4,128)S(1)} %get-tuple-element.39), channel_id=1, source_target_pairs={{0,1},{1,0},{2,3},{3,2},{4,5},{5,4},{6,7},{7,6},{8,9},{9,8},{10,11... | collective-permute-start | bytes 1544 | tf_op jit(solution)/shard_map/ppermute | solution.py:452
  62.6 4.6 %collective-permute-start.12 = (f32[1,4,32]{2,1,0:T(4,128)S(1)}, f32[1,4,32]{2,1,0:T(4,128)S(1)}, u32[]{:S(2)}, u32[]{:S(2)}) collective-permute-start(f32[1,4,32]{2,1,0:T(4,128)S(1)} %add.17), channel_id=1, source_target_pairs={{0,2},{1,3},{2,0},{3,1},{4,6},{5,7},{6,4},{7,5},{8,10},{9,11},{10,... | collective-permute-start | bytes 1544 | tf_op jit(solution)/shard_map/ppermute | solution.py:452
